TPU v7x, 256 devices: a whole 4x4x8 slice. The times are simulated.
256 devices in a mesh: slab: 4 (over y), strip: 64 (over z, x, core).
Axes of the slice: x: 4, y: 4, z: 8, core: 2. Of those that a mesh axis runs over, the one named last changes fastest.
Arguments:
- object_field: float32 [2, 8, 1024, 2048], P(None, 'slab', 'strip'), may hold values from -0.5 to 1.5
- first_moment: float32 [2, 8, 1024, 2048], P(None, 'slab', 'strip'), may hold values from -1.8 to 1.8
- second_moment: float32 [2, 8, 1024, 2048], P(None, 'slab', 'strip'), may hold values from 0.001 to 0.1
- probe_wave: float32 [2, 128, 128], replicated, may hold values from -6 to 6
- measured: float32 [256, 128, 128], P('strip'), may hold values from 0 to 4
- positions: int32 [256, 2], replicated, may hold values from 0 to 2047, as said below
- fresnel: float32 [1], replicated, may hold values from 0.002 to 0.02
Outputs:
- object_new: float32 [2, 8, 1024, 2048], P(None, 'slab', 'strip')
- first_new: float32 [2, 8, 1024, 2048], P(None, 'slab', 'strip')
- second_new: float32 [2, 8, 1024, 2048], P(None, 'slab', 'strip')
Inputs may be any that keep to these rules, and one draw needn't show every extreme that they name: `positions`: rows 4 d to 4 d + 3 hold (row, column) offsets whose row lies in object rows 16 d to 16 d + 15, for every d; columns lie in 0 to 2047.
All inputs are finite; a program needn't handle non-finite values.
Results may differ from a plain program's by a relative error of at most 0.0003.
Values sent between devices are 32-bit elements; how exact they have to be, the bound alone decides.
A program may use at most 64 MiB of HBM per device.

v0:
```python
import jax
import jax.numpy as jnp
from jax import lax
from jax.sharding import PartitionSpec as P

beta_one = 0.9
beta_two = 0.999
learn_rate = 0.05
adam_eps = 1e-08
adam_step = 10.0


def passed_along(x, axis, by):
    length = lax.axis_size(axis)
    return lax.ppermute(x, axis, [(i, (i + by) % length) for i in range(length)])


def matmul(left, right):
    return jnp.dot(left, right, precision=lax.Precision.HIGHEST)


def dft_tables(fresnel, patch_width):
    freq_index = jnp.arange(patch_width, dtype=jnp.int32)
    product = freq_index[:, None] * freq_index[None, :] % patch_width
    phase_angle = 2.0 * jnp.pi / patch_width * product.astype(jnp.float32)
    norm_scale = 1.0 / jnp.sqrt(jnp.asarray(patch_width, jnp.float32))
    four_real = jnp.cos(phase_angle) * norm_scale
    four_imag = -jnp.sin(phase_angle) * norm_scale
    signed = jnp.where(freq_index < patch_width // 2, freq_index, freq_index - patch_width).astype(
        jnp.float32
    )
    fresnel_phase = fresnel[0] * signed * signed
    kernel_real = jnp.cos(fresnel_phase)
    kernel_imag = -jnp.sin(fresnel_phase)
    left_real = four_real * kernel_real[None, :] + four_imag * kernel_imag[None, :]
    left_imag = four_real * kernel_imag[None, :] - four_imag * kernel_real[None, :]
    prop_real = matmul(left_real, four_real) - matmul(left_imag, four_imag)
    prop_imag = matmul(left_real, four_imag) + matmul(left_imag, four_real)
    return (four_real, four_imag, prop_real, prop_imag)


def complex_mul(left, right):
    left_real, left_imag = (left[..., 0, :, :], left[..., 1, :, :])
    right_real, right_imag = (right[..., 0, :, :], right[..., 1, :, :])
    return jnp.stack(
        [
            left_real * right_real - left_imag * right_imag,
            left_real * right_imag + left_imag * right_real,
        ],
        axis=-3,
    )


def conjugate(wave_field):
    return jnp.stack([wave_field[..., 0, :, :], -wave_field[..., 1, :, :]], axis=-3)


def apply_left(mat_real, mat_imag, wave_field):
    field_real, field_imag = (wave_field[..., 0, :, :], wave_field[..., 1, :, :])
    highest = lax.Precision.HIGHEST
    out_real = jnp.einsum("jk,...kl->...jl", mat_real, field_real, precision=highest) - jnp.einsum(
        "jk,...kl->...jl", mat_imag, field_imag, precision=highest
    )
    out_imag = jnp.einsum("jk,...kl->...jl", mat_real, field_imag, precision=highest) + jnp.einsum(
        "jk,...kl->...jl", mat_imag, field_real, precision=highest
    )
    return jnp.stack([out_real, out_imag], axis=-3)


def apply_right(wave_field, mat_real, mat_imag):
    field_real, field_imag = (wave_field[..., 0, :, :], wave_field[..., 1, :, :])
    highest = lax.Precision.HIGHEST
    out_real = jnp.einsum("...jk,kl->...jl", field_real, mat_real, precision=highest) - jnp.einsum(
        "...jk,kl->...jl", field_imag, mat_imag, precision=highest
    )
    out_imag = jnp.einsum("...jk,kl->...jl", field_real, mat_imag, precision=highest) + jnp.einsum(
        "...jk,kl->...jl", field_imag, mat_real, precision=highest
    )
    return jnp.stack([out_real, out_imag], axis=-3)


def propagate(tables, wave_field):
    four_real, four_imag, prop_real, prop_imag = tables
    return apply_right(apply_left(prop_real, prop_imag, wave_field), prop_real.T, prop_imag.T)


def propagate_adjoint(tables, wave_grad):
    four_real, four_imag, prop_real, prop_imag = tables
    return apply_right(apply_left(prop_real.T, -prop_imag.T, wave_grad), prop_real, -prop_imag)


def far_gradient(tables, exit_waves, measured):
    four_real, four_imag, prop_real, prop_imag = tables
    far_wave = apply_right(apply_left(four_real, four_imag, exit_waves), four_real, four_imag)
    intensity = far_wave[:, 0] * far_wave[:, 0] + far_wave[:, 1] * far_wave[:, 1]
    scaled = far_wave * (2.0 * (intensity - measured))[:, None]
    return apply_right(apply_left(four_real, -four_imag, scaled), four_real, -four_imag)


def section_forward(tables, entering, layers):
    saved_fields = []
    wave_field = entering
    for slice_index in range(layers.shape[2]):
        saved_fields.append(wave_field)
        wave_field = propagate(tables, complex_mul(wave_field, layers[:, :, slice_index]))
    return (wave_field, jnp.stack(saved_fields, axis=0))


def section_backward(tables, incoming, saved_fields, layers):
    wave_grad = incoming
    collected = []
    for slice_index in reversed(range(layers.shape[2])):
        mixed_grad = propagate_adjoint(tables, wave_grad)
        collected.append(complex_mul(conjugate(saved_fields[slice_index]), mixed_grad))
        wave_grad = complex_mul(conjugate(layers[:, :, slice_index]), mixed_grad)
    return (wave_grad, jnp.stack(collected[::-1], axis=2))


def fold_columns(widened, col_count):
    extra_cols = widened[..., col_count:]
    padding = [(0, 0)] * (widened.ndim - 1) + [(0, col_count - extra_cols.shape[-1])]
    return widened[..., :col_count] + jnp.pad(extra_cols, padding)


def adam_update(object_field, first_moment, second_moment, gradient):
    first_new = beta_one * first_moment + (1.0 - beta_one) * gradient
    second_new = beta_two * second_moment + (1.0 - beta_two) * gradient * gradient
    first_hat = first_new / (1.0 - beta_one**adam_step)
    second_hat = second_new / (1.0 - beta_two**adam_step)
    object_new = object_field - learn_rate * first_hat / (jnp.sqrt(second_hat) + adam_eps)
    return (object_new, first_new, second_new)


def shards(object_field, first_moment, second_moment, probe_wave, measured, positions, fresnel):
    patch_width = probe_wave.shape[-1]
    slice_count = object_field.shape[1]
    strip_rows = object_field.shape[2]
    col_count = object_field.shape[3]
    per_device = measured.shape[0]
    reach_strips = patch_width // strip_rows
    strip_index = lax.axis_index("strip")
    zero_index = jnp.zeros((), jnp.int32)
    tables = dft_tables(fresnel, patch_width)
    own_offsets = lax.dynamic_slice_in_dim(positions, strip_index * per_device, per_device, 0)
    local_rows = own_offsets[:, 0] - strip_index * strip_rows
    own_cols = own_offsets[:, 1]
    tall_count = (reach_strips + 1) * strip_rows
    pieces = [object_field]
    for distance in range(1, reach_strips + 1):
        pieces.append(passed_along(object_field, "strip", -distance))
    tall_rows = jnp.concatenate(pieces, axis=2)
    widened = jnp.concatenate([tall_rows, tall_rows[..., :patch_width]], axis=3)

    def cut_patch(start_row, start_col):
        return lax.dynamic_slice(
            widened,
            (zero_index, zero_index, start_row, start_col),
            (2, slice_count, patch_width, patch_width),
        )

    patches = jax.vmap(cut_patch)(local_rows, own_cols)
    slabs = lax.axis_size("slab")
    slab_index = lax.axis_index("slab")
    local_count = per_device // slabs
    gathered = lax.all_to_all(patches, "slab", split_axis=0, concat_axis=2, tiled=True)
    own_measured = lax.dynamic_slice_in_dim(measured, slab_index * local_count, local_count, 0)
    local_wave = jnp.broadcast_to(probe_wave, (local_count, 2, patch_width, patch_width))
    leaving, saved_fields = section_forward(tables, local_wave, gathered)
    exit_grad = far_gradient(tables, leaving, own_measured)
    passing, slice_grads = section_backward(tables, exit_grad, saved_fields, gathered)
    patch_grads = lax.all_to_all(slice_grads, "slab", split_axis=2, concat_axis=0, tiled=True)

    def add_patch(item_index, tall_rows):
        start = (zero_index, zero_index, local_rows[item_index], own_cols[item_index])
        current = lax.dynamic_slice(tall_rows, start, (2, slice_count, patch_width, patch_width))
        return lax.dynamic_update_slice(tall_rows, current + patch_grads[item_index], start)

    tall_rows = jnp.zeros((2, slice_count, tall_count, col_count + patch_width), jnp.float32)
    tall_rows = lax.fori_loop(0, per_device, add_patch, tall_rows)
    folded = fold_columns(tall_rows, col_count)
    gradient = folded[:, :, :strip_rows]
    for distance in range(1, reach_strips + 1):
        piece = folded[:, :, distance * strip_rows : (distance + 1) * strip_rows]
        gradient = gradient + passed_along(piece, "strip", distance)
    return adam_update(object_field, first_moment, second_moment, gradient)


def solution(mesh):
    return jax.shard_map(
        shards,
        mesh=mesh,
        in_specs=(
            P(None, "slab", "strip", None),
            P(None, "slab", "strip", None),
            P(None, "slab", "strip", None),
            P(),
            P("strip", None, None),
            P(),
            P(),
        ),
        out_specs=(
            P(None, "slab", "strip", None),
            P(None, "slab", "strip", None),
            P(None, "slab", "strip", None),
        ),
        check_vma=False,
    )
```

profile of v0, /device:TPU:1, one launch (start us, length us, event | category | flops | bytes accessed | tf_op | source)
XLA Modules:
  0.0 361.8 jit_solution(14491303706033775173)
XLA Ops:
  0.6 3.3 collective-permute-start
  3.9 6.1 %collective-permute-start.1 = (f32[2,2,16,2048]{3,2,1,0:T(8,128)}, f32[2,2,16,2048]{3,2,1,0:T(8,128)S(1)}, u32[]{:S(2)}, u32[]{:S(2)}) collective-permute-start(f32[2,2,16,2048]{3,2,1,0:T(8,128)} %param.9), channel_id=1, source_target_pairs={{0,62},{1,63},{2,0},{3,1},{4,2},{5,3},{6,4},{7,5},{8,6},{9,7},{10,... | collective-permute-start | bytes 1572872 | tf_op jit(solution)/shard_map/ppermute | solution.py:15
  10.0 0.8 collective-permute-start.2
  10.8 2.8 collective-permute-start.3
  13.6 0.9 collective-permute-start.4
  14.5 1.9 constant_dynamic-update-slice_fusion.8
  17.6 4.5 %collective-permute-done = f32[2,2,16,2048]{3,2,1,0:T(8,128)S(1)} collective-permute-done((f32[2,2,16,2048]{3,2,1,0:T(8,128)}, f32[2,2,16,2048]{3,2,1,0:T(8,128)S(1)}, u32[]{:S(2)}, u32[]{:S(2)}) %collective-permute-start) | collective-permute-done | bytes 524320 | tf_op jit(solution)/shard_map/ppermute | solution.py:15
  22.4 0.9 constant_dynamic-update-slice_fusion.7
  23.3 7.1 %collective-permute-done.1 = f32[2,2,16,2048]{3,2,1,0:T(8,128)S(1)} collective-permute-done((f32[2,2,16,2048]{3,2,1,0:T(8,128)}, f32[2,2,16,2048]{3,2,1,0:T(8,128)S(1)}, u32[]{:S(2)}, u32[]{:S(2)}) %collective-permute-start.1) | collective-permute-done | bytes 524320 | tf_op jit(solution)/shard_map/ppermute | solution.py:15
  30.4 19.4 %collective-permute-start.6 = (f32[2,2,16,2048]{3,2,1,0:T(8,128)}, f32[2,2,16,2048]{3,2,1,0:T(8,128)S(1)}, u32[]{:S(2)}, u32[]{:S(2)}) collective-permute-start(f32[2,2,16,2048]{3,2,1,0:T(8,128)} %param.9), channel_id=1, source_target_pairs={{0,57},{1,58},{2,59},{3,60},{4,61},{5,62},{6,63},{7,0},{8,1},{9,2}... | collective-permute-start | bytes 1572872 | tf_op jit(solution)/shard_map/ppermute | solution.py:15
  49.8 0.9 constant_dynamic-update-slice_fusion.6
  51.2 5.2 %collective-permute-start.7 = (f32[2,2,16,2048]{3,2,1,0:T(8,128)}, f32[2,2,16,2048]{3,2,1,0:T(8,128)S(1)}, u32[]{:S(2)}, u32[]{:S(2)}) collective-permute-start(f32[2,2,16,2048]{3,2,1,0:T(8,128)} %param.9), channel_id=1, source_target_pairs={{0,56},{1,57},{2,58},{3,59},{4,60},{5,61},{6,62},{7,63},{8,0},{9,1... | collective-permute-start | bytes 1572872 | tf_op jit(solution)/shard_map/ppermute | solution.py:15
  56.5 0.8 constant_dynamic-update-slice_fusion.5
  57.3 11.1 %collective-permute-done.3 = f32[2,2,16,2048]{3,2,1,0:T(8,128)S(1)} collective-permute-done((f32[2,2,16,2048]{3,2,1,0:T(8,128)}, f32[2,2,16,2048]{3,2,1,0:T(8,128)S(1)}, u32[]{:S(2)}, u32[]{:S(2)}) %collective-permute-start.3) | collective-permute-done | bytes 524320 | tf_op jit(solution)/shard_map/ppermute | solution.py:15
  68.4 0.9 constant_dynamic-update-slice_fusion.4
  69.3 21.9 %collective-permute-done.4 = f32[2,2,16,2048]{3,2,1,0:T(8,128)S(1)} collective-permute-done((f32[2,2,16,2048]{3,2,1,0:T(8,128)}, f32[2,2,16,2048]{3,2,1,0:T(8,128)S(1)}, u32[]{:S(2)}, u32[]{:S(2)}) %collective-permute-start.4) | collective-permute-done | bytes 524320 | tf_op jit(solution)/shard_map/ppermute | solution.py:15
  91.2 0.9 constant_dynamic-update-slice_fusion.3
  92.0 12.4 %collective-permute-done.5 = f32[2,2,16,2048]{3,2,1,0:T(8,128)S(1)} collective-permute-done((f32[2,2,16,2048]{3,2,1,0:T(8,128)}, f32[2,2,16,2048]{3,2,1,0:T(8,128)S(1)}, u32[]{:S(2)}, u32[]{:S(2)}) %collective-permute-start.5) | collective-permute-done | bytes 524320 | tf_op jit(solution)/shard_map/ppermute | solution.py:15
  104.4 0.9 constant_dynamic-update-slice_fusion.2
  105.3 19.7 %collective-permute-done.6 = f32[2,2,16,2048]{3,2,1,0:T(8,128)S(1)} collective-permute-done((f32[2,2,16,2048]{3,2,1,0:T(8,128)}, f32[2,2,16,2048]{3,2,1,0:T(8,128)S(1)}, u32[]{:S(2)}, u32[]{:S(2)}) %collective-permute-start.6) | collective-permute-done | bytes 524320 | tf_op jit(solution)/shard_map/ppermute | solution.py:15
  125.0 0.8 constant_dynamic-update-slice_fusion.1
  125.8 1.1 collective-permute-done.7
  126.9 0.9 constant_dynamic-update-slice_fusion
  127.8 1.0 slice.211
  128.8 5.0 %pad_maximum_fusion = f32[2,2,144,2176]{3,2,1,0:T(8,128)} fusion(f32[2,2,144,128]{3,2,1,0:T(8,128)S(1)} %slice.211, f32[2,2,144,2048]{3,2,1,0:T(8,128)} %constant_dynamic-update-slice_fusion), kind=kLoop, calls=%fused_computation.3 | loop fusion | flops 1253376 | bytes 10027008 | tf_op jit(solution)/shard_map/concatenate | solution.py:152
  133.8 15.3 %while.15 = (s32[]{:T(128)}, f32[2,2,144,2176]{3,2,1,0:T(8,128)}, s32[4,4]{1,0:T(4,128)S(1)}, f32[4,2,2,128,128]{4,3,2,1,0:T(8,128)}, s32[]{:T(128)}) while((s32[]{:T(128)}, f32[2,2,144,2176]{3,2,1,0:T(8,128)}, s32[4,4]{1,0:T(4,128)S(1)}, f32[4,2,2,128,128]{4,3,2,1,0:T(8,128)}, s32[]{:T(128)}) %tuple.110), condition=%wide.while_cond, body=%wide.while_body.sunk | while | flops 2 | bytes 525937 | solution.py:155
  134.4 3.2 bitcast_dynamic-update-slice_fusion.2
  138.2 3.2 bitcast_dynamic-update-slice_fusion.2
  142.0 3.2 bitcast_dynamic-update-slice_fusion.2
  145.9 3.2 bitcast_dynamic-update-slice_fusion.2
  149.1 4.5 %all-to-all-start = ((f32[4,2,2,128,128]{4,3,2,1,0:T(8,128)}), f32[4,2,2,128,128]{4,3,2,1,0:T(8,128)S(1)}, u32[]{:S(2)}, u32[]{:S(2)}) async-start(f32[4,2,2,128,128]{4,3,2,1,0:T(8,128)} %get-tuple-element.105), calls=%async_computation | async-start | bytes 2097152 | tf_op jit(solution)/shard_map/all_to_all | solution.py:165
  155.5 7.6 %all-to-all-done = f32[4,2,2,128,128]{4,3,2,1,0:T(8,128)S(1)} async-done(((f32[4,2,2,128,128]{4,3,2,1,0:T(8,128)}), f32[4,2,2,128,128]{4,3,2,1,0:T(8,128)S(1)}, u32[]{:S(2)}, u32[]{:S(2)}) %all-to-all-start) | async-done | bytes 1048608 | tf_op jit(solution)/shard_map/all_to_all | solution.py:165
  179.2 0.7 convolution_subtract_fusion.22
  186.4 0.9 fusion.56
  210.3 0.7 fusion.44
  210.9 0.7 fusion.45
  212.2 0.7 fusion.47
  212.9 0.7 fusion.48
  213.6 0.7 fusion.49
  214.2 0.7 fusion.50
  214.9 0.7 fusion.51
  215.6 3.5 all-to-all-start.1
  219.1 9.7 %all-to-all-done.1 = f32[1,2,8,128,128]{4,3,1,0,2:T(8,128)S(1)} async-done(((f32[1,2,8,128,128]{4,3,1,0,2:T(8,128)}), f32[1,2,8,128,128]{4,3,1,0,2:T(8,128)S(1)}, u32[]{:S(2)}, u32[]{:S(2)}) %all-to-all-start.1) | async-done | bytes 1048608 | tf_op jit(solution)/shard_map/all_to_all | solution.py:171
  228.9 2.6 broadcast_in_dim.4
  231.5 41.4 %while.14 = (s32[]{:T(128)}, f32[2,2,144,2176]{3,2,1,0:T(8,128)}, s32[4]{0:T(128)S(1)}, s32[4]{0:T(128)S(1)}, f32[4,2,2,128,128]{4,3,2,1,0:T(8,128)S(1)}, /*index=5*/s32[]{:T(128)}, s32[]{:T(128)}, s32[]{:T(128)}, s32[]{:T(128)}) while((s32[]{:T(128)}, f32[2,2,144,2176]{3,2,1,0:T(8,128)}, s32[4]{0:T(128)S(1)}, s32[4]{0:T(128)S(1)}, ...), condition=%wide.region_1.2_spmd, body=%wide.region_0.1_spmd.sunk | while | flops 65544 | bytes 1310921 | solution.py:179
  236.5 1.2 bitcast_add_fusion.2
  237.8 4.1 %dynamic_update_slice.8 = f32[2,2,144,2176]{3,2,1,0:T(8,128)} dynamic-update-slice(f32[2,2,144,2176]{3,2,1,0:T(8,128)} %get-tuple-element.304, f32[2,2,128,128]{3,2,1,0:T(8,128)S(1)} %bitcast_add_fusion.2, s32[]{:T(128)} %constant.80.clone.1..sunk, s32[]{:T(128)} %constant.80.clone.1..sunk, s32[]{:T(128)S(6)} %select_n.173, s32[]{:T(128)S(6)} %select_n.174) | dynamic-update-slice | bytes 524292 | tf_op jit(solution)/shard_map/while/body/eval_jaxpr/dynamic_update_slice | solution.py:176
  247.0 1.2 bitcast_add_fusion.2
  248.2 4.0 %dynamic_update_slice.8 = f32[2,2,144,2176]{3,2,1,0:T(8,128)} dynamic-update-slice(f32[2,2,144,2176]{3,2,1,0:T(8,128)} %get-tuple-element.304, f32[2,2,128,128]{3,2,1,0:T(8,128)S(1)} %bitcast_add_fusion.2, s32[]{:T(128)} %constant.80.clone.1..sunk, s32[]{:T(128)} %constant.80.clone.1..sunk, s32[]{:T(128)S(6)} %select_n.173, s32[]{:T(128)S(6)} %select_n.174) | dynamic-update-slice | bytes 524292 | tf_op jit(solution)/shard_map/while/body/eval_jaxpr/dynamic_update_slice | solution.py:176
  257.2 1.2 bitcast_add_fusion.2
  258.5 4.0 %dynamic_update_slice.8 = f32[2,2,144,2176]{3,2,1,0:T(8,128)} dynamic-update-slice(f32[2,2,144,2176]{3,2,1,0:T(8,128)} %get-tuple-element.304, f32[2,2,128,128]{3,2,1,0:T(8,128)S(1)} %bitcast_add_fusion.2, s32[]{:T(128)} %constant.80.clone.1..sunk, s32[]{:T(128)} %constant.80.clone.1..sunk, s32[]{:T(128)S(6)} %select_n.173, s32[]{:T(128)S(6)} %select_n.174) | dynamic-update-slice | bytes 524292 | tf_op jit(solution)/shard_map/while/body/eval_jaxpr/dynamic_update_slice | solution.py:176
  267.6 1.2 bitcast_add_fusion.2
  268.8 4.1 %dynamic_update_slice.8 = f32[2,2,144,2176]{3,2,1,0:T(8,128)} dynamic-update-slice(f32[2,2,144,2176]{3,2,1,0:T(8,128)} %get-tuple-element.304, f32[2,2,128,128]{3,2,1,0:T(8,128)S(1)} %bitcast_add_fusion.2, s32[]{:T(128)} %constant.80.clone.1..sunk, s32[]{:T(128)} %constant.80.clone.1..sunk, s32[]{:T(128)S(6)} %select_n.173, s32[]{:T(128)S(6)} %select_n.174) | dynamic-update-slice | bytes 524292 | tf_op jit(solution)/shard_map/while/body/eval_jaxpr/dynamic_update_slice | solution.py:176
  272.9 1.0 slice.181
  273.8 2.7 pad_add_fusion
  277.2 11.2 %collective-permute-start.11 = (f32[2,2,16,2048]{3,2,1,0:T(8,128)S(1)}, f32[2,2,16,2048]{3,2,1,0:T(8,128)S(1)}, u32[]{:S(2)}, u32[]{:S(2)}) collective-permute-start(f32[2,2,16,2048]{3,2,1,0:T(8,128)S(1)} %get-tuple-element.134), channel_id=1, source_target_pairs={{0,4},{1,5},{2,6},{3,7},{4,8},{5,9},{6,10},{7,11},{8,12},{9,13},{1... | collective-permute-start | bytes 1572872 | tf_op jit(solution)/shard_map/ppermute | solution.py:15
  288.4 2.2 collective-permute-start.13
  290.6 2.7 collective-permute-done.10
  293.4 1.3 collective-permute-start.15
  294.7 19.5 %collective-permute-done.11 = f32[2,2,16,2048]{3,2,1,0:T(8,128)S(1)} collective-permute-done((f32[2,2,16,2048]{3,2,1,0:T(8,128)S(1)}, f32[2,2,16,2048]{3,2,1,0:T(8,128)S(1)}, u32[]{:S(2)}, u32[]{:S(2)}) %collective-permute-start.11) | collective-permute-done | bytes 524320 | tf_op jit(solution)/shard_map/ppermute | solution.py:15
  314.2 1.2 collective-permute-done.12
  316.5 3.8 %collective-permute-done.8 = f32[2,2,16,2048]{3,2,1,0:T(8,128)S(1)} collective-permute-done((f32[2,2,16,2048]{3,2,1,0:T(8,128)S(1)}, f32[2,2,16,2048]{3,2,1,0:T(8,128)S(1)}, u32[]{:S(2)}, u32[]{:S(2)}) %collective-permute-start.8) | collective-permute-done | bytes 524320 | tf_op jit(solution)/shard_map/ppermute | solution.py:15
  320.3 39.5 %collective-permute-done.9 = f32[2,2,16,2048]{3,2,1,0:T(8,128)S(1)} collective-permute-done((f32[2,2,16,2048]{3,2,1,0:T(8,128)S(1)}, f32[2,2,16,2048]{3,2,1,0:T(8,128)S(1)}, u32[]{:S(2)}, u32[]{:S(2)}) %collective-permute-start.9) | collective-permute-done | bytes 524320 | tf_op jit(solution)/shard_map/ppermute | solution.py:15
  359.8 1.8 divide_subtract_fusion
  (201 shorter events, 57.3 us)
Async XLA Ops:
  0.6 16.4 %copy-start = (s32[256,2]{0,1:T(2,128)S(1)}, s32[256,2]{0,1:T(2,128)}, u32[]{:S(2)}) copy-start(s32[256,2]{0,1:T(2,128)} %param.14) | copy-start | bytes 6148
  0.6 21.5 %collective-permute-start = (f32[2,2,16,2048]{3,2,1,0:T(8,128)}, f32[2,2,16,2048]{3,2,1,0:T(8,128)S(1)}, u32[]{:S(2)}, u32[]{:S(2)}) collective-permute-start(f32[2,2,16,2048]{3,2,1,0:T(8,128)} %param.9), channel_id=1, source_target_pairs={{0,63},{1,0},{2,1},{3,2},{4,3},{5,4},{6,5},{7,6},{8,7},{9,8},{10,9... | collective-permute-start | bytes 1572872 | tf_op jit(solution)/shard_map/ppermute | solution.py:15
  3.9 26.4 %collective-permute-start.1 = (f32[2,2,16,2048]{3,2,1,0:T(8,128)}, f32[2,2,16,2048]{3,2,1,0:T(8,128)S(1)}, u32[]{:S(2)}, u32[]{:S(2)}) collective-permute-start(f32[2,2,16,2048]{3,2,1,0:T(8,128)} %param.9), channel_id=1, source_target_pairs={{0,62},{1,63},{2,0},{3,1},{4,2},{5,3},{6,4},{7,5},{8,6},{9,7},{10,... | collective-permute-start | bytes 1572872 | tf_op jit(solution)/shard_map/ppermute | solution.py:15
  10.0 41.2 %collective-permute-start.2 = (f32[2,2,16,2048]{3,2,1,0:T(8,128)}, f32[2,2,16,2048]{3,2,1,0:T(8,128)S(1)}, u32[]{:S(2)}, u32[]{:S(2)}) collective-permute-start(f32[2,2,16,2048]{3,2,1,0:T(8,128)} %param.9), channel_id=1, source_target_pairs={{0,61},{1,62},{2,63},{3,0},{4,1},{5,2},{6,3},{7,4},{8,5},{9,6},{10... | collective-permute-start | bytes 1572872 | tf_op jit(solution)/shard_map/ppermute | solution.py:15
  10.8 57.6 %collective-permute-start.3 = (f32[2,2,16,2048]{3,2,1,0:T(8,128)}, f32[2,2,16,2048]{3,2,1,0:T(8,128)S(1)}, u32[]{:S(2)}, u32[]{:S(2)}) collective-permute-start(f32[2,2,16,2048]{3,2,1,0:T(8,128)} %param.9), channel_id=1, source_target_pairs={{0,60},{1,61},{2,62},{3,63},{4,0},{5,1},{6,2},{7,3},{8,4},{9,5},{1... | collective-permute-start | bytes 1572872 | tf_op jit(solution)/shard_map/ppermute | solution.py:15
  13.6 77.6 %collective-permute-start.4 = (f32[2,2,16,2048]{3,2,1,0:T(8,128)}, f32[2,2,16,2048]{3,2,1,0:T(8,128)S(1)}, u32[]{:S(2)}, u32[]{:S(2)}) collective-permute-start(f32[2,2,16,2048]{3,2,1,0:T(8,128)} %param.9), channel_id=1, source_target_pairs={{0,59},{1,60},{2,61},{3,62},{4,63},{5,0},{6,1},{7,2},{8,3},{9,4},{... | collective-permute-start | bytes 1572872 | tf_op jit(solution)/shard_map/ppermute | solution.py:15
  22.1 82.3 %collective-permute-start.5 = (f32[2,2,16,2048]{3,2,1,0:T(8,128)}, f32[2,2,16,2048]{3,2,1,0:T(8,128)S(1)}, u32[]{:S(2)}, u32[]{:S(2)}) collective-permute-start(f32[2,2,16,2048]{3,2,1,0:T(8,128)} %param.9), channel_id=1, source_target_pairs={{0,58},{1,59},{2,60},{3,61},{4,62},{5,63},{6,0},{7,1},{8,2},{9,3},... | collective-permute-start | bytes 1572872 | tf_op jit(solution)/shard_map/ppermute | solution.py:15
  30.4 94.6 %collective-permute-start.6 = (f32[2,2,16,2048]{3,2,1,0:T(8,128)}, f32[2,2,16,2048]{3,2,1,0:T(8,128)S(1)}, u32[]{:S(2)}, u32[]{:S(2)}) collective-permute-start(f32[2,2,16,2048]{3,2,1,0:T(8,128)} %param.9), channel_id=1, source_target_pairs={{0,57},{1,58},{2,59},{3,60},{4,61},{5,62},{6,63},{7,0},{8,1},{9,2}... | collective-permute-start | bytes 1572872 | tf_op jit(solution)/shard_map/ppermute | solution.py:15
  51.2 75.7 %collective-permute-start.7 = (f32[2,2,16,2048]{3,2,1,0:T(8,128)}, f32[2,2,16,2048]{3,2,1,0:T(8,128)S(1)}, u32[]{:S(2)}, u32[]{:S(2)}) collective-permute-start(f32[2,2,16,2048]{3,2,1,0:T(8,128)} %param.9), channel_id=1, source_target_pairs={{0,56},{1,57},{2,58},{3,59},{4,60},{5,61},{6,62},{7,63},{8,0},{9,1... | collective-permute-start | bytes 1572872 | tf_op jit(solution)/shard_map/ppermute | solution.py:15
  149.1 14.2 %copy-start.4 = (f32[2,128,128]{2,1,0:T(8,128)S(1)}, f32[2,128,128]{2,1,0:T(8,128)}, u32[]{:S(2)}) copy-start(f32[2,128,128]{2,1,0:T(8,128)} %param.12) | copy-start | bytes 393220
  149.1 14.1 %all-to-all-start = ((f32[4,2,2,128,128]{4,3,2,1,0:T(8,128)}), f32[4,2,2,128,128]{4,3,2,1,0:T(8,128)S(1)}, u32[]{:S(2)}, u32[]{:S(2)}) async-start(f32[4,2,2,128,128]{4,3,2,1,0:T(8,128)} %get-tuple-element.105), calls=%async_computation | async-start | bytes 2097152 | tf_op jit(solution)/shard_map/all_to_all | solution.py:165
  215.6 13.2 %all-to-all-start.1 = ((f32[1,2,8,128,128]{4,3,1,0,2:T(8,128)}), f32[1,2,8,128,128]{4,3,1,0,2:T(8,128)S(1)}, u32[]{:S(2)}, u32[]{:S(2)}) async-start(f32[1,2,8,128,128]{4,3,1,0,2:T(8,128)} %bitcast.244), calls=%async_computation.1 | async-start | bytes 2097152 | tf_op jit(solution)/shard_map/all_to_all | solution.py:171
  276.6 83.3 %copy-start.1 = (f32[2,2,16,2048]{3,2,1,0:T(8,128)S(1)}, f32[2,2,16,2048]{3,2,1,0:T(8,128)}, u32[]{:S(2)}) copy-start(f32[2,2,16,2048]{3,2,1,0:T(8,128)} %param.9) | copy-start | bytes 1572868
  276.6 83.3 %copy-start.2 = (f32[2,2,16,2048]{3,2,1,0:T(8,128)S(1)}, f32[2,2,16,2048]{3,2,1,0:T(8,128)}, u32[]{:S(2)}) copy-start(f32[2,2,16,2048]{3,2,1,0:T(8,128)} %param.10) | copy-start | bytes 1572868
  276.6 83.3 %copy-start.3 = (f32[2,2,16,2048]{3,2,1,0:T(8,128)S(1)}, f32[2,2,16,2048]{3,2,1,0:T(8,128)}, u32[]{:S(2)}) copy-start(f32[2,2,16,2048]{3,2,1,0:T(8,128)} %param.11) | copy-start | bytes 1572868
  277.1 16.3 %collective-permute-start.10 = (f32[2,2,16,2048]{3,2,1,0:T(8,128)S(1)}, f32[2,2,16,2048]{3,2,1,0:T(8,128)S(1)}, u32[]{:S(2)}, u32[]{:S(2)}) collective-permute-start(f32[2,2,16,2048]{3,2,1,0:T(8,128)S(1)} %get-tuple-element.135), channel_id=1, source_target_pairs={{0,3},{1,4},{2,5},{3,6},{4,7},{5,8},{6,9},{7,10},{8,11},{9,12},{10... | collective-permute-start | bytes 1572872 | tf_op jit(solution)/shard_map/ppermute | solution.py:15
  277.2 37.0 %collective-permute-start.11 = (f32[2,2,16,2048]{3,2,1,0:T(8,128)S(1)}, f32[2,2,16,2048]{3,2,1,0:T(8,128)S(1)}, u32[]{:S(2)}, u32[]{:S(2)}) collective-permute-start(f32[2,2,16,2048]{3,2,1,0:T(8,128)S(1)} %get-tuple-element.134), channel_id=1, source_target_pairs={{0,4},{1,5},{2,6},{3,7},{4,8},{5,9},{6,10},{7,11},{8,12},{9,13},{1... | collective-permute-start | bytes 1572872 | tf_op jit(solution)/shard_map/ppermute | solution.py:15
  288.4 26.9 %collective-permute-start.12 = (f32[2,2,16,2048]{3,2,1,0:T(8,128)S(1)}, f32[2,2,16,2048]{3,2,1,0:T(8,128)S(1)}, u32[]{:S(2)}, u32[]{:S(2)}) collective-permute-start(f32[2,2,16,2048]{3,2,1,0:T(8,128)S(1)} %get-tuple-element.133), channel_id=1, source_target_pairs={{0,5},{1,6},{2,7},{3,8},{4,9},{5,10},{6,11},{7,12},{8,13},{9,14},{... | collective-permute-start | bytes 1572872 | tf_op jit(solution)/shard_map/ppermute | solution.py:15
  288.4 27.4 %collective-permute-start.13 = (f32[2,2,16,2048]{3,2,1,0:T(8,128)S(1)}, f32[2,2,16,2048]{3,2,1,0:T(8,128)S(1)}, u32[]{:S(2)}, u32[]{:S(2)}) collective-permute-start(f32[2,2,16,2048]{3,2,1,0:T(8,128)S(1)} %get-tuple-element.132), channel_id=1, source_target_pairs={{0,6},{1,7},{2,8},{3,9},{4,10},{5,11},{6,12},{7,13},{8,14},{9,15},... | collective-permute-start | bytes 1572872 | tf_op jit(solution)/shard_map/ppermute | solution.py:15
  290.6 25.8 %collective-permute-start.14 = (f32[2,2,16,2048]{3,2,1,0:T(8,128)S(1)}, f32[2,2,16,2048]{3,2,1,0:T(8,128)S(1)}, u32[]{:S(2)}, u32[]{:S(2)}) collective-permute-start(f32[2,2,16,2048]{3,2,1,0:T(8,128)S(1)} %get-tuple-element.131), channel_id=1, source_target_pairs={{0,7},{1,8},{2,9},{3,10},{4,11},{5,12},{6,13},{7,14},{8,15},{9,16}... | collective-permute-start | bytes 1572872 | tf_op jit(solution)/shard_map/ppermute | solution.py:15
  293.4 23.1 %collective-permute-start.15 = (f32[2,2,16,2048]{3,2,1,0:T(8,128)S(1)}, f32[2,2,16,2048]{3,2,1,0:T(8,128)S(1)}, u32[]{:S(2)}, u32[]{:S(2)}) collective-permute-start(f32[2,2,16,2048]{3,2,1,0:T(8,128)S(1)} %get-tuple-element.130), channel_id=1, source_target_pairs={{0,8},{1,9},{2,10},{3,11},{4,12},{5,13},{6,14},{7,15},{8,16},{9,17... | collective-permute-start | bytes 1572872 | tf_op jit(solution)/shard_map/ppermute | solution.py:15
  314.2 6.1 %collective-permute-start.8 = (f32[2,2,16,2048]{3,2,1,0:T(8,128)S(1)}, f32[2,2,16,2048]{3,2,1,0:T(8,128)S(1)}, u32[]{:S(2)}, u32[]{:S(2)}) collective-permute-start(f32[2,2,16,2048]{3,2,1,0:T(8,128)S(1)} %get-tuple-element.129), channel_id=1, source_target_pairs={{0,1},{1,2},{2,3},{3,4},{4,5},{5,6},{6,7},{7,8},{8,9},{9,10},{10,1... | collective-permute-start | bytes 1572872 | tf_op jit(solution)/shard_map/ppermute | solution.py:15
  315.3 44.5 %collective-permute-start.9 = (f32[2,2,16,2048]{3,2,1,0:T(8,128)S(1)}, f32[2,2,16,2048]{3,2,1,0:T(8,128)S(1)}, u32[]{:S(2)}, u32[]{:S(2)}) collective-permute-start(f32[2,2,16,2048]{3,2,1,0:T(8,128)S(1)} %get-tuple-element.136), channel_id=1, source_target_pairs={{0,2},{1,3},{2,4},{3,5},{4,6},{5,7},{6,8},{7,9},{8,10},{9,11},{10,... | collective-permute-start | bytes 1572872 | tf_op jit(solution)/shard_map/ppermute | solution.py:15
where the time goes:
time: 369 us; the launch traced here: 362 us
  waiting for transfers between devices  163 us (44%)
  starting transfers between devices  62.1 us (17%)
  local copies, waits for them, and re-layouts  50.6 us (14%)
  matrix products  46.9 us (13%)
  other arithmetic  20.8 us (6%)
  loops' own time  15.6 us (4%)
    ppermute x16, waiting for transfers between devices, passed_along(): lax.ppermute(x, axis, [(i, (i + by) % length) for i in range(length)])  146 us
    ppermute x16, starting transfers between devices, passed_along(): lax.ppermute(x, axis, [(i, (i + by) % length) for i in range(length)])  54.1 us
    dynamic_update_slice x4, local copies, waits for them, and re-layouts, add_patch(): lax.dynamic_update_slice(tall_rows, current + patch_grads[item_index], st...  16.3 us
    another operation x1, loops' own time, shards(): tall_rows = lax.fori_loop(0, per_device, add_patch, tall_rows)  15.6 us
    gather x12, local copies, waits for them, and re-layouts  15.3 us
    all_to_all x1, waiting for transfers between devices, shards(): lax.all_to_all(slice_grads, 'slab', split_axis=2, concat_axis=0, tiled=True)  9.71 us
    unnamed x20, local copies, waits for them, and re-layouts  8.13 us
    all_to_all x1, waiting for transfers between devices, shards(): lax.all_to_all(patches, 'slab', split_axis=0, concat_axis=2, tiled=True)  7.65 us
  transfers between devices with their start and end apart: 18, of which 16 were waited for; matrix products, arithmetic and copies ran while one was open for 3% of the time, Pallas kernels for 0%

commit v1 on v0

v1 whole, which is shorter than its diff:
```python
import functools

import jax
import jax.numpy as jnp
import numpy as np
from jax import lax
from jax.experimental import pallas as pl
from jax.experimental.pallas import tpu as pltpu
from jax.sharding import PartitionSpec as P

beta_one = 0.9
beta_two = 0.999
learn_rate = 0.05
adam_eps = 1e-08
adam_step = 10.0

PATCH = 128
ROWS = 16
SPAN = PATCH // ROWS
REACH = SPAN + 1
MESH = pl.DeviceIdType.MESH


def fourier_table():
    index = np.arange(PATCH)
    angle = 2.0 * np.pi / PATCH * ((index[:, None] * index[None, :]) % PATCH)
    table = np.stack([np.cos(angle), -np.sin(angle)]) / np.sqrt(PATCH)
    return jnp.asarray(table.astype(np.float32))


def split(value):
    high = value.astype(jnp.bfloat16)
    low = (value - high.astype(jnp.float32)).astype(jnp.bfloat16)
    return high, low


def rolled(value, amount, axis, bits):
    for bit in range(bits):
        taken = jnp.broadcast_to((amount >> bit) & 1, value.shape) == 1
        value = jnp.where(taken, pltpu.roll(value, 1 << bit, axis), value)
    return value


def dot(left, right):
    return jnp.dot(left, right, preferred_element_type=jnp.float32)


def both_sides(tab, left, right, real, imag):
    high, low = split(jnp.concatenate([real, imag], axis=1))
    wide = dot(jnp.concatenate([high, low], axis=0), tab[right, 0])
    fine = dot(high, tab[right, 1])
    turned = wide[:PATCH] + wide[PATCH:] + fine
    high, low = split(jnp.concatenate([turned[:, :PATCH], turned[:, PATCH:]], axis=0))
    wide = dot(tab[left, 0], jnp.concatenate([high, low], axis=1))
    fine = dot(tab[left, 1], high)
    done = wide[:, :PATCH] + wide[:, PATCH:] + fine
    return done[:PATCH], done[PATCH:]


def fill_tables(tab, four, fresnel):
    four_real, four_imag = four[0], four[1]

    def phase(axis):
        index = lax.broadcasted_iota(jnp.int32, (PATCH, PATCH), axis)
        signed = jnp.where(index < PATCH // 2, index, index - PATCH).astype(jnp.float32)
        angle = fresnel * signed * signed
        return jnp.cos(angle), -jnp.sin(angle)

    def scaled(axis):
        real, imag = phase(axis)
        return four_real * real - four_imag * imag, four_real * imag + four_imag * real

    def put(slot, real, imag, sign):
        top = jnp.concatenate([real, -imag if sign > 0 else imag], axis=1)
        bottom = jnp.concatenate([imag if sign > 0 else -imag, real], axis=1)
        high, low = split(jnp.concatenate([top, bottom], axis=0))
        tab[slot, 0] = high
        tab[slot, 1] = low

    def full(left, right):
        return jnp.dot(
            left, right, precision=lax.Precision.HIGHEST, preferred_element_type=jnp.float32
        )

    far_real, far_imag = scaled(0)
    put(2, far_real, far_imag, 1)
    prop_real = full(four_real, far_real) + full(four_imag, far_imag)
    prop_imag = full(four_real, far_imag) - full(four_imag, far_real)
    put(0, prop_real, prop_imag, 1)
    put(1, prop_real, prop_imag, -1)
    put(3, *scaled(1), -1)


def wave_kernel(
    slabs, strips, pos, fresnel, obj_in, probe_in, meas_in, four_in, out,
    obj, probe, meas, four, stage, recv, tab, saved, waves, gst,
    tile_sem, load_sem, patch_send, patch_recv, grad_send, grad_recv, own_sem,
):
    me_slab = lax.axis_index("slab")
    me_strip = lax.axis_index("strip")
    count = REACH * slabs

    def below(j):
        return lax.rem(me_strip + strips - j, strips)

    def above(j):
        return lax.rem(me_strip + j, strips)

    tiles = obj.shape[0]

    def tile_load(t):
        return pltpu.make_async_copy(
            obj_in.at[:, :, :, pl.ds(pl.multiple_of(t * PATCH, PATCH), PATCH)], obj.at[t], tile_sem.at[t]
        )

    def start_tile(t, carry):
        tile_load(t).start()
        return carry

    def wait_tile(t, carry):
        tile_load(t).wait()
        return carry

    lax.fori_loop(0, tiles, start_tile, 0)
    loads = [
        pltpu.make_async_copy(probe_in, probe, load_sem.at[0]),
        pltpu.make_async_copy(meas_in.at[me_slab], meas, load_sem.at[1]),
        pltpu.make_async_copy(four_in, four, load_sem.at[2]),
    ]
    for load in loads:
        load.start()

    barrier = pltpu.get_barrier_semaphore()

    def greet(i, carry):
        j = i // slabs
        peer = lax.rem(me_slab + lax.rem(i, slabs), slabs)

        @pl.when(i > 0)
        def _():
            pl.semaphore_signal(
                barrier, inc=1, device_id={"slab": peer, "strip": below(j)}, device_id_type=MESH
            )

        @pl.when(j > 0)
        def _():
            pl.semaphore_signal(
                barrier, inc=1, device_id={"slab": peer, "strip": above(j)}, device_id_type=MESH
            )

        return carry

    lax.fori_loop(0, count, greet, 0)
    lax.fori_loop(0, tiles, wait_tile, 0)
    lane = lax.broadcasted_iota(jnp.int32, (2, 2, ROWS, PATCH), 3)

    def cut(i, carry):
        j = i // slabs
        item = below(j) * slabs + lax.rem(i, slabs)
        column = pos[item, 1]
        tile = lax.shift_right_logical(column, 7)
        after = (tile + 1) & 15
        stage[i] = jnp.where(lane >= (column & 127), obj[tile], obj[after])
        return carry

    lax.fori_loop(0, count, cut, 0)
    pl.semaphore_wait(barrier, 2 * count - slabs - 1)

    def patch_copy(i):
        j = i // slabs
        peer = lax.rem(me_slab + lax.rem(i, slabs), slabs)
        return pltpu.make_async_remote_copy(
            src_ref=stage.at[j * slabs + peer],
            dst_ref=recv.at[me_slab, j],
            send_sem=patch_send.at[i],
            recv_sem=patch_recv.at[me_slab, j],
            device_id={"slab": peer, "strip": below(j)},
            device_id_type=MESH,
        )

    def send_patch(i, carry):
        patch_copy(i).start()
        return carry

    lax.fori_loop(1, count, send_patch, 0)
    recv[me_slab, 0] = stage[me_slab]

    for load in loads:
        load.wait()
    fill_tables(tab, four, fresnel[0])
    own = me_strip * slabs + me_slab
    own_row = pos[own, 0] - me_strip * ROWS
    own_shift = pos[own, 1] & 127
    for part in range(2):
        waves[part] = rolled(rolled(probe[part], own_row, 0, 4), own_shift, 1, 7)
    row = lax.broadcasted_iota(jnp.int32, (ROWS, PATCH), 0)

    def arrived(q):
        def one(j, carry):
            @pl.when((q != me_slab) | (j > 0))
            def _():
                pltpu.make_async_remote_copy(
                    src_ref=stage.at[0],
                    dst_ref=recv.at[q, j],
                    send_sem=patch_send.at[0],
                    recv_sem=patch_recv.at[q, j],
                    device_id={"slab": q, "strip": above(j)},
                    device_id_type=MESH,
                ).wait_recv()

            return carry

        lax.fori_loop(0, REACH, one, 0)

    def layer(s):
        q, n = s // 2, lax.rem(s, 2)
        parts = []
        for part in range(2):
            first = jnp.where(row >= own_row, recv[q, 0, part, n], recv[q, SPAN, part, n])
            rest = [recv[q, j, part, n] for j in range(1, SPAN)]
            parts.append(jnp.concatenate([first] + rest, axis=0))
        return parts

    def enter(s):
        real, imag = waves[0], waves[1]
        saved[s, 0] = real
        saved[s, 1] = imag
        layer_real, layer_imag = layer(s)
        return (
            real * layer_real - imag * layer_imag,
            real * layer_imag + imag * layer_real,
        )

    def forward(s, carry):
        @pl.when(lax.rem(s, 2) == 0)
        def _():
            arrived(s // 2)

        real, imag = both_sides(tab, 0, 1, *enter(s))
        waves[0] = real
        waves[1] = imag
        return carry

    slices = 2 * slabs
    lax.fori_loop(0, slices - 1, forward, 0)
    real, imag = both_sides(tab, 2, 3, *enter(slices - 1))
    factor = 2.0 * (real * real + imag * imag - meas[...])
    real, imag = both_sides(tab, 3, 2, real * factor, imag * factor)
    waves[0] = real
    waves[1] = imag

    def leave(s):
        q, n = s // 2, lax.rem(s, 2)
        real, imag = waves[0], waves[1]
        old_real, old_imag = saved[s, 0], saved[s, 1]
        grad_real = old_real * real + old_imag * imag
        grad_imag = old_real * imag - old_imag * real
        for j in range(SPAN):
            gst[q, j, 0, n] = grad_real[j * ROWS : (j + 1) * ROWS]
            gst[q, j, 1, n] = grad_imag[j * ROWS : (j + 1) * ROWS]

    def grad_copy(q, j):
        return pltpu.make_async_remote_copy(
            src_ref=gst.at[q, lax.rem(j, SPAN)],
            dst_ref=out.at[j, me_slab],
            send_sem=grad_send.at[q, j],
            recv_sem=grad_recv.at[j, me_slab],
            device_id={"slab": q, "strip": above(j)},
            device_id_type=MESH,
        )

    own_copy = pltpu.make_async_copy(gst.at[me_slab, 0], out.at[0, me_slab], own_sem)

    def send_grads(q):
        def one(j, carry):
            @pl.when((q != me_slab) | (j > 0))
            def _():
                grad_copy(q, j).start()

            return carry

        lax.fori_loop(0, REACH, one, 0)

        @pl.when(q == me_slab)
        def _():
            own_copy.start()

    def backward(i, carry):
        s = slices - 1 - i
        leave(s)

        @pl.when(lax.rem(s, 2) == 0)
        def _():
            send_grads(s // 2)

        real, imag = waves[0], waves[1]
        layer_real, layer_imag = layer(s)
        real, imag = both_sides(
            tab, 1, 0,
            layer_real * real + layer_imag * imag,
            layer_real * imag - layer_imag * real,
        )
        waves[0] = real
        waves[1] = imag
        return carry

    lax.fori_loop(0, slices - 1, backward, 0)
    leave(0)
    send_grads(0)

    def finish_patch(i, carry):
        patch_copy(i).wait_send()
        return carry

    lax.fori_loop(1, count, finish_patch, 0)

    def finish_grad(i, carry):
        j, q = i // slabs, lax.rem(i, slabs)

        @pl.when((q != me_slab) | (j > 0))
        def _():
            grad_copy(q, j).wait_send()
            pltpu.make_async_remote_copy(
                src_ref=gst.at[q, 0],
                dst_ref=out.at[j, q],
                send_sem=grad_send.at[q, j],
                recv_sem=grad_recv.at[j, q],
                device_id={"slab": q, "strip": below(j)},
                device_id_type=MESH,
            ).wait_recv()

        return carry

    lax.fori_loop(0, count, finish_grad, 0)
    own_copy.wait()


def update_kernel(slabs, strips, pos, pieces, obj, first, second, obj_out, first_out, second_out, grad):
    me_strip = lax.axis_index("strip")
    grad[...] = jnp.zeros_like(grad)
    shape = (2, 2, ROWS, PATCH)
    lane = lax.broadcasted_iota(jnp.int32, shape, 3)
    row = lax.broadcasted_iota(jnp.int32, shape, 2)

    def place(i, carry):
        j, k = i // slabs, lax.rem(i, slabs)
        owner = lax.rem(me_strip + strips - j, strips)
        item = owner * slabs + k
        column = pos[item, 1]
        local_row = pos[item, 0] - owner * ROWS
        low = jnp.where(j == 0, local_row, 0)
        high = jnp.where(j == SPAN, local_row, ROWS)
        tile = lax.shift_right_logical(column, 7)
        after = (tile + 1) & 15
        shift = column & 127
        piece = jnp.where((row >= low) & (row < high), pieces[j, k], 0.0)
        here = pl.ds(pl.multiple_of(tile * PATCH, PATCH), PATCH)
        there = pl.ds(pl.multiple_of(after * PATCH, PATCH), PATCH)
        grad[:, :, :, here] += jnp.where(lane >= shift, piece, 0.0)
        grad[:, :, :, there] += jnp.where(lane >= shift, 0.0, piece)
        return carry

    lax.fori_loop(0, REACH * slabs, place, 0)
    gradient = grad[...]
    first_new = beta_one * first[...] + (1.0 - beta_one) * gradient
    second_new = beta_two * second[...] + (1.0 - beta_two) * gradient * gradient
    first_hat = first_new / (1.0 - beta_one**adam_step)
    second_hat = second_new / (1.0 - beta_two**adam_step)
    obj_out[...] = obj[...] - learn_rate * first_hat / (jnp.sqrt(second_hat) + adam_eps)
    first_out[...] = first_new
    second_out[...] = second_new


def shards(slabs, strips, object_field, first_moment, second_moment, probe_wave, measured, positions, fresnel):
    vmem = pl.BlockSpec(memory_space=pltpu.VMEM)
    smem = pl.BlockSpec(memory_space=pltpu.SMEM)
    anywhere = pl.BlockSpec(memory_space=pl.ANY)
    f32 = jnp.float32
    count = REACH * slabs
    tiles = object_field.shape[3] // PATCH
    piece = (2, 2, ROWS, PATCH)
    pair = (2, PATCH, PATCH)
    pieces = pl.pallas_call(
        functools.partial(wave_kernel, slabs, strips),
        out_shape=jax.ShapeDtypeStruct((REACH, slabs) + piece, f32),
        in_specs=[smem, smem, anywhere, anywhere, anywhere, anywhere],
        out_specs=anywhere,
        scratch_shapes=[
            pltpu.VMEM((tiles,) + piece, f32),
            pltpu.VMEM(pair, f32),
            pltpu.VMEM((PATCH, PATCH), f32),
            pltpu.VMEM(pair, f32),
            pltpu.VMEM((count,) + piece, f32),
            pltpu.VMEM((slabs, REACH) + piece, f32),
            pltpu.VMEM((4, 2, 2 * PATCH, 2 * PATCH), jnp.bfloat16),
            pltpu.VMEM((2 * slabs,) + pair, f32),
            pltpu.VMEM(pair, f32),
            pltpu.VMEM((slabs, SPAN) + piece, f32),
            pltpu.SemaphoreType.DMA((tiles,)),
            pltpu.SemaphoreType.DMA((3,)),
            pltpu.SemaphoreType.DMA((count,)),
            pltpu.SemaphoreType.DMA((slabs, REACH)),
            pltpu.SemaphoreType.DMA((slabs, REACH)),
            pltpu.SemaphoreType.DMA((REACH, slabs)),
            pltpu.SemaphoreType.DMA(()),
        ],
        compiler_params=pltpu.CompilerParams(collective_id=0, has_side_effects=True),
    )(positions, fresnel, object_field, probe_wave, measured, fourier_table())
    like = jax.ShapeDtypeStruct(object_field.shape, f32)
    return pl.pallas_call(
        functools.partial(update_kernel, slabs, strips),
        out_shape=(like, like, like),
        in_specs=[smem, vmem, vmem, vmem, vmem],
        out_specs=(vmem, vmem, vmem),
        scratch_shapes=[pltpu.VMEM(object_field.shape, f32)],
    )(positions, pieces, object_field, first_moment, second_moment)


def solution(mesh):
    spec = P(None, "slab", "strip", None)
    return jax.shard_map(
        functools.partial(shards, mesh.shape["slab"], mesh.shape["strip"]),
        mesh=mesh,
        in_specs=(spec, spec, spec, P(), P("strip", None, None), P(), P()),
        out_specs=(spec, spec, spec),
        check_vma=False,
    )
```

time: 369 us -> 74.2 us (0.20); the launches traced: 362 us -> 74 us
  waiting for transfers between devices: 163 us -> 0 us
  Pallas kernels: 0 us -> 71.3 us
  starting transfers between devices: 62.1 us -> 0 us
  local copies, waits for them, and re-layouts: 50.6 us -> 1.47 us
  matrix products: 46.9 us -> 0 us
  other arithmetic: 20.8 us -> 0 us
  loops' own time: 15.6 us -> 0 us
    ppermute x16 -> x0, waiting for transfers between devices: 146 us -> none  [passed_along(): lax.ppermute(x, axis, [(i, (i + by) % length) for i in range(length)])]
    pallas_call x0 -> x2, Pallas kernels: none -> 71.3 us  [the longest x1 65.8 us: shards(): pl.pallas_call(functools.partial(wave_kernel, slabs, strips), out_shape=j...]
    ppermute x16 -> x0, starting transfers between devices: 54.1 us -> none  [passed_along(): lax.ppermute(x, axis, [(i, (i + by) % length) for i in range(length)])]
    dot_general x148 -> x0, matrix products: 46.9 us -> none  [the longest x18 5.98 us: apply_right(): jnp.einsum('...jk,kl->...jl', field_imag, mat_imag, precision=highest)]
    all_to_all x2 -> x0, waiting for transfers between devices: 17.4 us -> none  [the longest x1 9.71 us: shards(): lax.all_to_all(slice_grads, 'slab', split_axis=2, concat_axis=0, tiled=True)]
    dynamic_update_slice x4 -> x0, local copies, waits for them, and re-layouts: 16.3 us -> none  [add_patch(): lax.dynamic_update_slice(tall_rows, current + patch_grads[item_index], st...]
    another operation x2 -> x0, loops' own time: 15.6 us -> none  [the longest x1 15.6 us: shards(): tall_rows = lax.fori_loop(0, per_device, add_patch, tall_rows)]
    gather x12 -> x0, local copies, waits for them, and re-layouts: 15.3 us -> none
  transfers between devices with their start and end apart: 18 -> 0, of which waited for: 16 -> 0; matrix products, arithmetic and copies ran while one was open for 3% -> 0% of each run, Pallas kernels for 0% -> 0%
where the time goes in v1:
time: 74.2 us; the launch traced here: 74 us
  Pallas kernels  71.3 us (96%)
  local copies, waits for them, and re-layouts  1.47 us (2%)
  between operations  1.29 us (2%)
    pallas_call x1, Pallas kernels, shards(): pl.pallas_call(functools.partial(wave_kernel, slabs, strips), out_shape=j...  65.8 us
    pallas_call x1, Pallas kernels, shards(): pl.pallas_call(functools.partial(update_kernel, slabs, strips), out_shape...  5.42 us

profile of v1, /device:TPU:1, one launch (start us, length us, event | category | flops | bytes accessed | tf_op | source)
XLA Modules:
  0.0 74.0 jit_solution(2220843272357616203)
XLA Ops:
  1.3 1.5 %copy.12.pos = s32[256,2]{1,0:T(8,128)} copy(s32[256,2]{0,1:T(2,128)} %param.13) | data formatting | bytes 4096 | tf_op args[5]
  2.8 65.8 %shard_map.103.pieces = f32[9,4,2,2,16,128]{5,4,3,2,1,0:T(8,128)} custom-call(s32[256,2]{1,0:T(8,128)} %copy.12.pos, f32[1]{0:T(128)S(6)} %copy.13.fresnel, f32[2,2,16,2048]{3,2,1,0:T(8,128)} %obj.1, f32[2,128,128]{2,1,0:T(8,128)} %probe_in.1, f32[4,128,128]{2,1,0:T(8,128)} %meas_in.1, f32[2,128,128]{2,1,0:T(8,128)} %constant.2.clone.four_in), custom_call_target="tpu_custom_call" | custom-call | tf_op jit(solution)/shard_map/pallas_call | solution.py:383
  68.6 5.4 %shard_map.104 = (f32[2,2,16,2048]{3,2,1,0:T(8,128)}, f32[2,2,16,2048]{3,2,1,0:T(8,128)}, f32[2,2,16,2048]{3,2,1,0:T(8,128)}) custom-call(s32[256,2]{1,0:T(8,128)} %copy.12.pos, f32[9,4,2,2,16,128]{5,4,3,2,1,0:T(8,128)} %shard_map.103.pieces, f32[2,2,16,2048]{3,2,1,0:T(8,128)} %obj.1, f32[2,2,16,2048]{3,2,1,0:T(8,128)} %first.1, f32[2,2,16,2048]{3,2,1,0:T(8,128)} %second.1), custom_call_target="tpu_custom_call" | custom-call | tf_op jit(solution)/shard_map/pallas_call | solution.py:410

commit v2 on v1

--- a/solution.py
+++ b/solution.py
@@ -18,6 +18,7 @@
 ROWS = 16
 SPAN = PATCH // ROWS
 REACH = SPAN + 1
+CENTER = 4
 MESH = pl.DeviceIdType.MESH
 
 
@@ -92,19 +93,22 @@
 
 
 def wave_kernel(
-    slabs, strips, pos, fresnel, obj_in, probe_in, meas_in, four_in, out,
-    obj, probe, meas, four, stage, recv, tab, saved, waves, gst,
-    tile_sem, load_sem, patch_send, patch_recv, grad_send, grad_recv, own_sem,
+    slabs, strips, pos_in, fresnel_in, obj_in, probe_in, meas_in, four_in, out,
+    pos, fresnel, obj, probe, meas, four, stage, recv, tab, saved, waves, gst,
+    tile_sem, load_sem, meas_sem, patch_send, patch_recv, grad_send, grad_recv, own_sem,
 ):
     me_slab = lax.axis_index("slab")
     me_strip = lax.axis_index("strip")
     count = REACH * slabs
 
     def below(j):
-        return lax.rem(me_strip + strips - j, strips)
+        return lax.rem(me_strip + strips + CENTER - j, strips)
 
     def above(j):
-        return lax.rem(me_strip + j, strips)
+        return lax.rem(me_strip + strips - CENTER + j, strips)
+
+    def remote(peer, j):
+        return (peer != me_slab) | (j != CENTER)
 
     tiles = obj.shape[0]
 
@@ -121,11 +125,13 @@
         tile_load(t).wait()
         return carry
 
+    pos_load = pltpu.make_async_copy(pos_in, pos, load_sem.at[2])
+    pos_load.start()
     lax.fori_loop(0, tiles, start_tile, 0)
     loads = [
         pltpu.make_async_copy(probe_in, probe, load_sem.at[0]),
-        pltpu.make_async_copy(meas_in.at[me_slab], meas, load_sem.at[1]),
-        pltpu.make_async_copy(four_in, four, load_sem.at[2]),
+        pltpu.make_async_copy(four_in, four, load_sem.at[1]),
+        pltpu.make_async_copy(fresnel_in, fresnel, load_sem.at[3]),
     ]
     for load in loads:
         load.start()
@@ -134,70 +140,81 @@
 
     def greet(i, carry):
         j = i // slabs
-        peer = lax.rem(me_slab + lax.rem(i, slabs), slabs)
-
-        @pl.when(i > 0)
+        peer = lax.rem(i, slabs)
+
+        @pl.when(remote(peer, j))
         def _():
             pl.semaphore_signal(
                 barrier, inc=1, device_id={"slab": peer, "strip": below(j)}, device_id_type=MESH
             )
 
-        @pl.when(j > 0)
-        def _():
-            pl.semaphore_signal(
-                barrier, inc=1, device_id={"slab": peer, "strip": above(j)}, device_id_type=MESH
-            )
-
         return carry
 
     lax.fori_loop(0, count, greet, 0)
+    pos_load.wait()
     lax.fori_loop(0, tiles, wait_tile, 0)
     lane = lax.broadcasted_iota(jnp.int32, (2, 2, ROWS, PATCH), 3)
 
     def cut(i, carry):
         j = i // slabs
-        item = below(j) * slabs + lax.rem(i, slabs)
-        column = pos[item, 1]
+        item = lax.rem(me_strip + strips - j, strips) * slabs + lax.rem(i, slabs)
+        column = pos[1, item]
         tile = lax.shift_right_logical(column, 7)
         after = (tile + 1) & 15
         stage[i] = jnp.where(lane >= (column & 127), obj[tile], obj[after])
         return carry
 
     lax.fori_loop(0, count, cut, 0)
-    pl.semaphore_wait(barrier, 2 * count - slabs - 1)
-
-    def patch_copy(i):
-        j = i // slabs
-        peer = lax.rem(me_slab + lax.rem(i, slabs), slabs)
+    pl.semaphore_wait(barrier, count - 1)
+
+    def patch_copy(j, peer):
         return pltpu.make_async_remote_copy(
             src_ref=stage.at[j * slabs + peer],
             dst_ref=recv.at[me_slab, j],
-            send_sem=patch_send.at[i],
+            send_sem=patch_send.at[j * slabs + peer],
             recv_sem=patch_recv.at[me_slab, j],
             device_id={"slab": peer, "strip": below(j)},
             device_id_type=MESH,
         )
 
+    def patch_order(i):
+        return lax.rem(i, REACH), lax.rem(me_slab + i // REACH, slabs)
+
     def send_patch(i, carry):
-        patch_copy(i).start()
-        return carry
-
-    lax.fori_loop(1, count, send_patch, 0)
-    recv[me_slab, 0] = stage[me_slab]
+        j, peer = patch_order(i)
+
+        @pl.when(remote(peer, j))
+        def _():
+            patch_copy(j, peer).start()
+
+        return carry
+
+    lax.fori_loop(0, count, send_patch, 0)
+    meas_copy = pltpu.make_async_remote_copy(
+        src_ref=meas_in.at[me_slab],
+        dst_ref=meas,
+        send_sem=meas_sem.at[0],
+        recv_sem=meas_sem.at[1],
+        device_id={"slab": me_slab, "strip": below(0)},
+        device_id_type=MESH,
+    )
+    meas_copy.start()
+    recv[me_slab, CENTER] = stage[CENTER * slabs + me_slab]
 
     for load in loads:
         load.wait()
     fill_tables(tab, four, fresnel[0])
-    own = me_strip * slabs + me_slab
-    own_row = pos[own, 0] - me_strip * ROWS
-    own_shift = pos[own, 1] & 127
+    owner = lax.rem(me_strip + strips - CENTER, strips)
+    own = owner * slabs + me_slab
+    own_row = pos[0, own] - owner * ROWS
+    own_shift = pos[1, own] & 127
     for part in range(2):
         waves[part] = rolled(rolled(probe[part], own_row, 0, 4), own_shift, 1, 7)
     row = lax.broadcasted_iota(jnp.int32, (ROWS, PATCH), 0)
 
     def arrived(q):
         def one(j, carry):
-            @pl.when((q != me_slab) | (j > 0))
+            @pl.when(remote(q, j))
             def _():
                 pltpu.make_async_remote_copy(
                     src_ref=stage.at[0],
@@ -244,6 +261,7 @@
     slices = 2 * slabs
     lax.fori_loop(0, slices - 1, forward, 0)
     real, imag = both_sides(tab, 2, 3, *enter(slices - 1))
+    meas_copy.wait_recv()
     factor = 2.0 * (real * real + imag * imag - meas[...])
     real, imag = both_sides(tab, 3, 2, real * factor, imag * factor)
     waves[0] = real
@@ -269,11 +287,11 @@
             device_id_type=MESH,
         )
 
-    own_copy = pltpu.make_async_copy(gst.at[me_slab, 0], out.at[0, me_slab], own_sem)
+    own_copy = pltpu.make_async_copy(gst.at[me_slab, CENTER], out.at[CENTER, me_slab], own_sem)
 
     def send_grads(q):
         def one(j, carry):
-            @pl.when((q != me_slab) | (j > 0))
+            @pl.when(remote(q, j))
             def _():
                 grad_copy(q, j).start()
 
@@ -309,15 +327,21 @@
     send_grads(0)
 
     def finish_patch(i, carry):
-        patch_copy(i).wait_send()
-        return carry
-
-    lax.fori_loop(1, count, finish_patch, 0)
+        j, peer = patch_order(i)
+
+        @pl.when(remote(peer, j))
+        def _():
+            patch_copy(j, peer).wait_send()
+
+        return carry
+
+    lax.fori_loop(0, count, finish_patch, 0)
+    meas_copy.wait_send()
 
     def finish_grad(i, carry):
         j, q = i // slabs, lax.rem(i, slabs)
 
-        @pl.when((q != me_slab) | (j > 0))
+        @pl.when(remote(q, j))
         def _():
             grad_copy(q, j).wait_send()
             pltpu.make_async_remote_copy(
@@ -346,8 +370,8 @@
         j, k = i // slabs, lax.rem(i, slabs)
         owner = lax.rem(me_strip + strips - j, strips)
         item = owner * slabs + k
-        column = pos[item, 1]
-        local_row = pos[item, 0] - owner * ROWS
+        column = pos[1, item]
+        local_row = pos[0, item] - owner * ROWS
         low = jnp.where(j == 0, local_row, 0)
         high = jnp.where(j == SPAN, local_row, ROWS)
         tile = lax.shift_right_logical(column, 7)
@@ -380,12 +404,15 @@
     tiles = object_field.shape[3] // PATCH
     piece = (2, 2, ROWS, PATCH)
     pair = (2, PATCH, PATCH)
+    turned = positions.T
     pieces = pl.pallas_call(
         functools.partial(wave_kernel, slabs, strips),
         out_shape=jax.ShapeDtypeStruct((REACH, slabs) + piece, f32),
-        in_specs=[smem, smem, anywhere, anywhere, anywhere, anywhere],
+        in_specs=[pl.BlockSpec(memory_space=pltpu.HBM)] * 6,
         out_specs=anywhere,
         scratch_shapes=[
+            pltpu.SMEM((2, positions.shape[0]), jnp.int32),
+            pltpu.SMEM((1,), f32),
             pltpu.VMEM((tiles,) + piece, f32),
             pltpu.VMEM(pair, f32),
             pltpu.VMEM((PATCH, PATCH), f32),
@@ -397,15 +424,18 @@
             pltpu.VMEM(pair, f32),
             pltpu.VMEM((slabs, SPAN) + piece, f32),
             pltpu.SemaphoreType.DMA((tiles,)),
-            pltpu.SemaphoreType.DMA((3,)),
+            pltpu.SemaphoreType.DMA((4,)),
+            pltpu.SemaphoreType.DMA((2,)),
             pltpu.SemaphoreType.DMA((count,)),
             pltpu.SemaphoreType.DMA((slabs, REACH)),
             pltpu.SemaphoreType.DMA((slabs, REACH)),
             pltpu.SemaphoreType.DMA((REACH, slabs)),
             pltpu.SemaphoreType.DMA(()),
         ],
-        compiler_params=pltpu.CompilerParams(collective_id=0, has_side_effects=True),
-    )(positions, fresnel, object_field, probe_wave, measured, fourier_table())
+        compiler_params=pltpu.CompilerParams(
+            collective_id=0, has_side_effects=True, vmem_limit_bytes=62 << 20
+        ),
+    )(turned, fresnel, object_field, probe_wave, measured, fourier_table())
     like = jax.ShapeDtypeStruct(object_field.shape, f32)
     return pl.pallas_call(
         functools.partial(update_kernel, slabs, strips),
@@ -413,7 +443,8 @@
         in_specs=[smem, vmem, vmem, vmem, vmem],
         out_specs=(vmem, vmem, vmem),
         scratch_shapes=[pltpu.VMEM(object_field.shape, f32)],
-    )(positions, pieces, object_field, first_moment, second_moment)
+        compiler_params=pltpu.CompilerParams(vmem_limit_bytes=12 << 20),
+    )(turned, pieces, object_field, first_moment, second_moment)
 
 
 def solution(mesh):

time: 74.2 us -> 62.7 us (0.85)
  Pallas kernels: 71.3 us -> 59.9 us
    pallas_call x1, Pallas kernels: 65.8 us -> 56.8 us  [shards(): pl.pallas_call(functools.partial(wave_kernel, slabs, strips), out_shape=j...]
    pallas_call x1, Pallas kernels: 5.42 us -> 3.07 us  [shards(): pl.pallas_call(functools.partial(update_kernel, slabs, strips), out_shape...]
where the time goes in v2:
time: 62.7 us; the launch traced here: 62.6 us
  Pallas kernels  59.9 us (96%)
  between operations  1.47 us (2%)
  local copies, waits for them, and re-layouts  1.28 us (2%)
    pallas_call x1, Pallas kernels, shards(): pl.pallas_call(functools.partial(wave_kernel, slabs, strips), out_shape=j...  56.8 us
    pallas_call x1, Pallas kernels, shards(): pl.pallas_call(functools.partial(update_kernel, slabs, strips), out_shape...  3.07 us
    unnamed x10, local copies, waits for them, and re-layouts  1.28 us

profile of v2, /device:TPU:1, one launch (start us, length us, event | category | flops | bytes accessed | tf_op | source)
XLA Modules:
  0.0 62.6 jit_solution(2509601649306876347)
XLA Ops:
  0.6 0.0 copy-start.1
  0.6 0.0 copy-start.4
  0.7 0.0 copy-start.3
  0.7 0.0 copy-start.2
  1.4 56.8 %shard_map.103.pieces = f32[9,4,2,2,16,128]{5,4,3,2,1,0:T(8,128)} custom-call(s32[2,256]{1,0:T(2,128)} %bitcast.1, f32[1]{0:T(128)S(6)} %copy.11.fresnel_in, f32[2,2,16,2048]{3,2,1,0:T(8,128)} %obj.1, f32[2,128,128]{2,1,0:T(8,128)} %probe_in.1, f32[4,128,128]{2,1,0:T(8,128)} %meas_in.1, f32[2,128,128]{2,1,0:T(8,128)} %constant.2.clone.four_in), custom_call_target="tpu_custom_call" | custom-call | tf_op jit(solution)/shard_map/pallas_call | solution.py:408
  58.2 0.0 copy-done.1
  58.2 0.0 copy-done.4
  58.2 0.0 copy-done.3
  58.3 0.0 copy-done.2
  58.3 0.0 copy-start
  58.3 1.3 %copy-done = f32[9,4,2,2,16,128]{5,4,3,2,1,0:T(8,128)S(1)} copy-done((f32[9,4,2,2,16,128]{5,4,3,2,1,0:T(8,128)S(1)}, f32[9,4,2,2,16,128]{5,4,3,2,1,0:T(8,128)}, u32[]{:S(2)}) %copy-start) | copy-done | bytes 1179672
  59.5 3.1 %shard_map.104 = (f32[2,2,16,2048]{3,2,1,0:T(8,128)}, f32[2,2,16,2048]{3,2,1,0:T(8,128)}, f32[2,2,16,2048]{3,2,1,0:T(8,128)}) custom-call(s32[2,256]{1,0:T(2,128)S(1)} %bitcast.2, f32[9,4,2,2,16,128]{5,4,3,2,1,0:T(8,128)S(1)} %copy-done, f32[2,2,16,2048]{3,2,1,0:T(8,128)S(1)} %copy-done.1, f32[2,2,16,2048]{3,2,1,0:T(8,128)S(1)} %copy-done.2, ...), custom_call_target="tpu_custom_call" | custom-call | tf_op jit(solution)/shard_map/pallas_call | solution.py:440
Async XLA Ops:
  0.6 57.6 %copy-start.1 = (f32[2,2,16,2048]{3,2,1,0:T(8,128)S(1)}, f32[2,2,16,2048]{3,2,1,0:T(8,128)}, u32[]{:S(2)}) copy-start(f32[2,2,16,2048]{3,2,1,0:T(8,128)} %obj.1) | copy-start | bytes 1572868
  0.6 57.6 %copy-start.4 = (s32[256,2]{0,1:T(2,128)S(1)}, s32[256,2]{0,1:T(2,128)}, u32[]{:S(2)}) copy-start(s32[256,2]{0,1:T(2,128)} %param.13) | copy-start | bytes 6148
  0.7 57.6 %copy-start.3 = (f32[2,2,16,2048]{3,2,1,0:T(8,128)S(1)}, f32[2,2,16,2048]{3,2,1,0:T(8,128)}, u32[]{:S(2)}) copy-start(f32[2,2,16,2048]{3,2,1,0:T(8,128)} %second.1) | copy-start | bytes 1572868
  0.7 57.6 %copy-start.2 = (f32[2,2,16,2048]{3,2,1,0:T(8,128)S(1)}, f32[2,2,16,2048]{3,2,1,0:T(8,128)}, u32[]{:S(2)}) copy-start(f32[2,2,16,2048]{3,2,1,0:T(8,128)} %first.1) | copy-start | bytes 1572868
  58.3 1.3 %copy-start = (f32[9,4,2,2,16,128]{5,4,3,2,1,0:T(8,128)S(1)}, f32[9,4,2,2,16,128]{5,4,3,2,1,0:T(8,128)}, u32[]{:S(2)}) copy-start(f32[9,4,2,2,16,128]{5,4,3,2,1,0:T(8,128)} %shard_map.103.pieces) | copy-start | bytes 3538948

commit v3 on v2

--- a/solution.py
+++ b/solution.py
@@ -18,7 +18,8 @@
 ROWS = 16
 SPAN = PATCH // ROWS
 REACH = SPAN + 1
-CENTER = 4
+CENTER = SPAN // 2
+AHEAD = 6
 MESH = pl.DeviceIdType.MESH
 
 
@@ -101,11 +102,14 @@
     me_strip = lax.axis_index("strip")
     count = REACH * slabs
 
-    def below(j):
-        return lax.rem(me_strip + strips + CENTER - j, strips)
-
-    def above(j):
-        return lax.rem(me_strip + strips - CENTER + j, strips)
+    def moved(by):
+        return lax.rem(me_strip + strips + by, strips)
+
+    def worker(peer, j):
+        return {"slab": peer, "strip": moved(CENTER - j)}
+
+    def holder(peer, j):
+        return {"slab": peer, "strip": moved(j - CENTER)}
 
     def remote(peer, j):
         return (peer != me_slab) | (j != CENTER)
@@ -139,13 +143,12 @@
     barrier = pltpu.get_barrier_semaphore()
 
     def greet(i, carry):
-        j = i // slabs
-        peer = lax.rem(i, slabs)
+        j, peer = i // slabs, lax.rem(i, slabs)
 
         @pl.when(remote(peer, j))
         def _():
             pl.semaphore_signal(
-                barrier, inc=1, device_id={"slab": peer, "strip": below(j)}, device_id_type=MESH
+                barrier, inc=1, device_id=worker(peer, j), device_id_type=MESH
             )
 
         return carry
@@ -155,17 +158,20 @@
     lax.fori_loop(0, tiles, wait_tile, 0)
     lane = lax.broadcasted_iota(jnp.int32, (2, 2, ROWS, PATCH), 3)
 
-    def cut(i, carry):
-        j = i // slabs
-        item = lax.rem(me_strip + strips - j, strips) * slabs + lax.rem(i, slabs)
+    def patch_order(i):
+        return lax.rem(i, REACH), lax.rem(me_slab + i // REACH, slabs)
+
+    def cut(i):
+        j, peer = patch_order(i)
+        item = moved(-j) * slabs + peer
         column = pos[1, item]
         tile = lax.shift_right_logical(column, 7)
         after = (tile + 1) & 15
-        stage[i] = jnp.where(lane >= (column & 127), obj[tile], obj[after])
-        return carry
-
-    lax.fori_loop(0, count, cut, 0)
-    pl.semaphore_wait(barrier, count - 1)
+        stage[j * slabs + peer] = jnp.where(lane >= (column & 127), obj[tile], obj[after])
+
+    def cut_more(i, carry):
+        cut(i)
+        return carry
 
     def patch_copy(j, peer):
         return pltpu.make_async_remote_copy(
@@ -173,12 +179,9 @@
             dst_ref=recv.at[me_slab, j],
             send_sem=patch_send.at[j * slabs + peer],
             recv_sem=patch_recv.at[me_slab, j],
-            device_id={"slab": peer, "strip": below(j)},
+            device_id=worker(peer, j),
             device_id_type=MESH,
         )
-
-    def patch_order(i):
-        return lax.rem(i, REACH), lax.rem(me_slab + i // REACH, slabs)
 
     def send_patch(i, carry):
         j, peer = patch_order(i)
@@ -189,22 +192,31 @@
 
         return carry
 
-    lax.fori_loop(0, count, send_patch, 0)
-    meas_copy = pltpu.make_async_remote_copy(
+    lax.fori_loop(0, AHEAD, cut_more, 0)
+    pl.semaphore_wait(barrier, count - 1)
+
+    def cut_and_send(i, carry):
+        send_patch(i, carry)
+        cut(i + AHEAD)
+        return carry
+
+    lax.fori_loop(0, count - AHEAD, cut_and_send, 0)
+    lax.fori_loop(count - AHEAD, count, send_patch, 0)
+    far_meas = pltpu.make_async_remote_copy(
         src_ref=meas_in.at[me_slab],
         dst_ref=meas,
         send_sem=meas_sem.at[0],
         recv_sem=meas_sem.at[1],
-        device_id={"slab": me_slab, "strip": below(0)},
+        device_id={"slab": me_slab, "strip": moved(CENTER)},
         device_id_type=MESH,
     )
-    meas_copy.start()
+    far_meas.start()
     recv[me_slab, CENTER] = stage[CENTER * slabs + me_slab]
 
     for load in loads:
         load.wait()
     fill_tables(tab, four, fresnel[0])
-    owner = lax.rem(me_strip + strips - CENTER, strips)
+    owner = moved(-CENTER)
     own = owner * slabs + me_slab
     own_row = pos[0, own] - owner * ROWS
     own_shift = pos[1, own] & 127
@@ -221,7 +233,7 @@
                     dst_ref=recv.at[q, j],
                     send_sem=patch_send.at[0],
                     recv_sem=patch_recv.at[q, j],
-                    device_id={"slab": q, "strip": above(j)},
+                    device_id=holder(q, j),
                     device_id_type=MESH,
                 ).wait_recv()
 
@@ -259,9 +271,10 @@
         return carry
 
     slices = 2 * slabs
-    lax.fori_loop(0, slices - 1, forward, 0)
+    lax.fori_loop(0, slices - 1, forward, 0, unroll=True)
     real, imag = both_sides(tab, 2, 3, *enter(slices - 1))
-    meas_copy.wait_recv()
+
+    far_meas.wait_recv()
     factor = 2.0 * (real * real + imag * imag - meas[...])
     real, imag = both_sides(tab, 3, 2, real * factor, imag * factor)
     waves[0] = real
@@ -283,11 +296,13 @@
             dst_ref=out.at[j, me_slab],
             send_sem=grad_send.at[q, j],
             recv_sem=grad_recv.at[j, me_slab],
-            device_id={"slab": q, "strip": above(j)},
+            device_id=holder(q, j),
             device_id_type=MESH,
         )
 
-    own_copy = pltpu.make_async_copy(gst.at[me_slab, CENTER], out.at[CENTER, me_slab], own_sem)
+    own_copy = pltpu.make_async_copy(
+        gst.at[me_slab, CENTER], out.at[CENTER, me_slab], own_sem
+    )
 
     def send_grads(q):
         def one(j, carry):
@@ -322,7 +337,7 @@
         waves[1] = imag
         return carry
 
-    lax.fori_loop(0, slices - 1, backward, 0)
+    lax.fori_loop(0, slices - 1, backward, 0, unroll=True)
     leave(0)
     send_grads(0)
 
@@ -336,7 +351,7 @@
         return carry
 
     lax.fori_loop(0, count, finish_patch, 0)
-    meas_copy.wait_send()
+    far_meas.wait_send()
 
     def finish_grad(i, carry):
         j, q = i // slabs, lax.rem(i, slabs)
@@ -349,7 +364,7 @@
                 dst_ref=out.at[j, q],
                 send_sem=grad_send.at[q, j],
                 recv_sem=grad_recv.at[j, q],
-                device_id={"slab": q, "strip": below(j)},
+                device_id=worker(q, j),
                 device_id_type=MESH,
             ).wait_recv()
 
@@ -407,9 +422,9 @@
     turned = positions.T
     pieces = pl.pallas_call(
         functools.partial(wave_kernel, slabs, strips),
-        out_shape=jax.ShapeDtypeStruct((REACH, slabs) + piece, f32),
+        out_shape=pltpu.VMEM((REACH, slabs) + piece, f32),
         in_specs=[pl.BlockSpec(memory_space=pltpu.HBM)] * 6,
-        out_specs=anywhere,
+        out_specs=pl.BlockSpec(memory_space=pltpu.VMEM),
         scratch_shapes=[
             pltpu.SMEM((2, positions.shape[0]), jnp.int32),
             pltpu.SMEM((1,), f32),
@@ -433,7 +448,7 @@
             pltpu.SemaphoreType.DMA(()),
         ],
         compiler_params=pltpu.CompilerParams(
-            collective_id=0, has_side_effects=True, vmem_limit_bytes=62 << 20
+            collective_id=0, has_side_effects=True, vmem_limit_bytes=61000000
         ),
     )(turned, fresnel, object_field, probe_wave, measured, fourier_table())
     like = jax.ShapeDtypeStruct(object_field.shape, f32)

time: 62.7 us -> 60.3 us (0.962)
  local copies, waits for them, and re-layouts: 1.28 us -> 0.02 us
  Pallas kernels: 59.9 us -> 58.8 us
    unnamed x10 -> x8, local copies, waits for them, and re-layouts: 1.28 us -> 0.02 us
    pallas_call x1, Pallas kernels: 56.8 us -> 55.7 us  [shards(): pl.pallas_call(functools.partial(wave_kernel, slabs, strips), out_shape=p...]
where the time goes in v3:
time: 60.3 us; the launch traced here: 60.2 us
  Pallas kernels  58.8 us (98%)
  between operations  1.46 us (2%)
    pallas_call x1, Pallas kernels, shards(): pl.pallas_call(functools.partial(wave_kernel, slabs, strips), out_shape=p...  55.7 us
    pallas_call x1, Pallas kernels, shards(): pl.pallas_call(functools.partial(update_kernel, slabs, strips), out_shape...  3.08 us

profile of v3, /device:TPU:1, one launch (start us, length us, event | category | flops | bytes accessed | tf_op | source)
XLA Modules:
  0.0 60.2 jit_solution(6201111611173533836)
XLA Ops:
  0.6 0.0 copy-start
  0.6 0.0 copy-start.3
  0.7 0.0 copy-start.2
  0.7 0.0 copy-start.1
  1.4 55.7 %shard_map.103.pieces = f32[9,4,2,2,16,128]{5,4,3,2,1,0:T(8,128)S(1)} custom-call(s32[2,256]{1,0:T(2,128)} %bitcast.1, f32[1]{0:T(128)S(6)} %copy.11.fresnel_in, f32[2,2,16,2048]{3,2,1,0:T(8,128)} %obj.1, f32[2,128,128]{2,1,0:T(8,128)} %probe_in.1, f32[4,128,128]{2,1,0:T(8,128)} %meas_in.1, f32[2,128,128]{2,1,0:T(8,128)} %constant.2.clone.four_in), custom_call_target="tpu_custom_call" | custom-call | tf_op jit(solution)/shard_map/pallas_call | solution.py:423
  57.1 0.0 copy-done
  57.1 0.0 copy-done.3
  57.1 0.0 copy-done.2
  57.1 0.0 copy-done.1
  57.2 3.1 %shard_map.104 = (f32[2,2,16,2048]{3,2,1,0:T(8,128)}, f32[2,2,16,2048]{3,2,1,0:T(8,128)}, f32[2,2,16,2048]{3,2,1,0:T(8,128)}) custom-call(s32[2,256]{1,0:T(2,128)S(1)} %bitcast.2, f32[9,4,2,2,16,128]{5,4,3,2,1,0:T(8,128)S(1)} %shard_map.103.pieces, f32[2,2,16,2048]{3,2,1,0:T(8,128)S(1)} %copy-done, f32[2,2,16,2048]{3,2,1,0:T(8,128)S(1)} %copy-done.1, ...), custom_call_target="tpu_custom_call" | custom-call | tf_op jit(solution)/shard_map/pallas_call | solution.py:455
Async XLA Ops:
  0.6 56.5 %copy-start = (f32[2,2,16,2048]{3,2,1,0:T(8,128)S(1)}, f32[2,2,16,2048]{3,2,1,0:T(8,128)}, u32[]{:S(2)}) copy-start(f32[2,2,16,2048]{3,2,1,0:T(8,128)} %obj.1) | copy-start | bytes 1572868
  0.6 56.5 %copy-start.3 = (s32[256,2]{0,1:T(2,128)S(1)}, s32[256,2]{0,1:T(2,128)}, u32[]{:S(2)}) copy-start(s32[256,2]{0,1:T(2,128)} %param.13) | copy-start | bytes 6148
  0.7 56.5 %copy-start.2 = (f32[2,2,16,2048]{3,2,1,0:T(8,128)S(1)}, f32[2,2,16,2048]{3,2,1,0:T(8,128)}, u32[]{:S(2)}) copy-start(f32[2,2,16,2048]{3,2,1,0:T(8,128)} %second.1) | copy-start | bytes 1572868
  0.7 56.5 %copy-start.1 = (f32[2,2,16,2048]{3,2,1,0:T(8,128)S(1)}, f32[2,2,16,2048]{3,2,1,0:T(8,128)}, u32[]{:S(2)}) copy-start(f32[2,2,16,2048]{3,2,1,0:T(8,128)} %first.1) | copy-start | bytes 1572868

commit v4 on v3

--- a/solution.py
+++ b/solution.py
@@ -374,7 +374,7 @@
     own_copy.wait()
 
 
-def update_kernel(slabs, strips, pos, pieces, obj, first, second, obj_out, first_out, second_out, grad):
+def update_kernel(slabs, strips, pos, pieces, obj, first, second, obj_out, first_out, second_out, grad, done, out_sem):
     me_strip = lax.axis_index("strip")
     grad[...] = jnp.zeros_like(grad)
     shape = (2, 2, ROWS, PATCH)
@@ -399,15 +399,29 @@
         grad[:, :, :, there] += jnp.where(lane >= shift, 0.0, piece)
         return carry
 
-    lax.fori_loop(0, REACH * slabs, place, 0)
-    gradient = grad[...]
-    first_new = beta_one * first[...] + (1.0 - beta_one) * gradient
-    second_new = beta_two * second[...] + (1.0 - beta_two) * gradient * gradient
-    first_hat = first_new / (1.0 - beta_one**adam_step)
-    second_hat = second_new / (1.0 - beta_two**adam_step)
-    obj_out[...] = obj[...] - learn_rate * first_hat / (jnp.sqrt(second_hat) + adam_eps)
-    first_out[...] = first_new
-    second_out[...] = second_new
+    lax.fori_loop(0, REACH * slabs, place, 0, unroll=4)
+    copies = []
+    for part in range(2):
+        for n in range(2):
+            gradient = grad[part, n]
+            first_new = beta_one * first[part, n] + (1.0 - beta_one) * gradient
+            second_new = beta_two * second[part, n] + (1.0 - beta_two) * gradient * gradient
+            first_hat = first_new / (1.0 - beta_one**adam_step)
+            second_hat = second_new / (1.0 - beta_two**adam_step)
+            done[0, part, n] = obj[part, n] - learn_rate * first_hat / (
+                jnp.sqrt(second_hat) + adam_eps
+            )
+            done[1, part, n] = first_new
+            done[2, part, n] = second_new
+            for slot, target in enumerate((obj_out, first_out, second_out)):
+                copies.append(
+                    pltpu.make_async_copy(
+                        done.at[slot, part, n], target.at[part, n], out_sem.at[slot, part, n]
+                    )
+                )
+                copies[-1].start()
+    for copy in copies:
+        copy.wait()
 
 
 def shards(slabs, strips, object_field, first_moment, second_moment, probe_wave, measured, positions, fresnel):
@@ -456,8 +470,12 @@
         functools.partial(update_kernel, slabs, strips),
         out_shape=(like, like, like),
         in_specs=[smem, vmem, vmem, vmem, vmem],
-        out_specs=(vmem, vmem, vmem),
-        scratch_shapes=[pltpu.VMEM(object_field.shape, f32)],
+        out_specs=(anywhere, anywhere, anywhere),
+        scratch_shapes=[
+            pltpu.VMEM(object_field.shape, f32),
+            pltpu.VMEM((3,) + object_field.shape, f32),
+            pltpu.SemaphoreType.DMA((3, 2, 2)),
+        ],
         compiler_params=pltpu.CompilerParams(vmem_limit_bytes=12 << 20),
     )(turned, pieces, object_field, first_moment, second_moment)
 

time: 60.3 us -> 60 us (level)
  no operation moved by 1% of the time
where the time goes in v4:
time: 60 us; the launch traced here: 59.9 us
  Pallas kernels  58.4 us (97%)
  between operations  1.46 us (2%)
    pallas_call x1, Pallas kernels, shards(): pl.pallas_call(functools.partial(wave_kernel, slabs, strips), out_shape=p...  55.7 us
    pallas_call x1, Pallas kernels, shards(): pl.pallas_call(functools.partial(update_kernel, slabs, strips), out_shape...  2.7 us

profile of v4, /device:TPU:1, one launch (start us, length us, event | category | flops | bytes accessed | tf_op | source)
XLA Modules:
  0.0 59.9 jit_solution(12976293398332017451)
XLA Ops:
  0.6 0.0 copy-start
  0.6 0.0 copy-start.3
  0.7 0.0 copy-start.2
  0.7 0.0 copy-start.1
  1.4 55.7 %shard_map.103.pieces = f32[9,4,2,2,16,128]{5,4,3,2,1,0:T(8,128)S(1)} custom-call(s32[2,256]{1,0:T(2,128)} %bitcast.1, f32[1]{0:T(128)S(6)} %copy.11.fresnel_in, f32[2,2,16,2048]{3,2,1,0:T(8,128)} %obj.1, f32[2,128,128]{2,1,0:T(8,128)} %probe_in.1, f32[4,128,128]{2,1,0:T(8,128)} %meas_in.1, f32[2,128,128]{2,1,0:T(8,128)} %constant.2.clone.four_in), custom_call_target="tpu_custom_call" | custom-call | tf_op jit(solution)/shard_map/pallas_call | solution.py:437
  57.1 0.0 copy-done
  57.1 0.0 copy-done.3
  57.1 0.0 copy-done.2
  57.1 0.0 copy-done.1
  57.2 2.7 %shard_map.104 = (f32[2,2,16,2048]{3,2,1,0:T(8,128)}, f32[2,2,16,2048]{3,2,1,0:T(8,128)}, f32[2,2,16,2048]{3,2,1,0:T(8,128)}) custom-call(s32[2,256]{1,0:T(2,128)S(1)} %bitcast.2, f32[9,4,2,2,16,128]{5,4,3,2,1,0:T(8,128)S(1)} %shard_map.103.pieces, f32[2,2,16,2048]{3,2,1,0:T(8,128)S(1)} %copy-done, f32[2,2,16,2048]{3,2,1,0:T(8,128)S(1)} %copy-done.1, ...), custom_call_target="tpu_custom_call" | custom-call | tf_op jit(solution)/shard_map/pallas_call | solution.py:469
Async XLA Ops:
  0.6 56.5 %copy-start = (f32[2,2,16,2048]{3,2,1,0:T(8,128)S(1)}, f32[2,2,16,2048]{3,2,1,0:T(8,128)}, u32[]{:S(2)}) copy-start(f32[2,2,16,2048]{3,2,1,0:T(8,128)} %obj.1) | copy-start | bytes 1572868
  0.6 56.5 %copy-start.3 = (s32[256,2]{0,1:T(2,128)S(1)}, s32[256,2]{0,1:T(2,128)}, u32[]{:S(2)}) copy-start(s32[256,2]{0,1:T(2,128)} %param.13) | copy-start | bytes 6148
  0.7 56.5 %copy-start.2 = (f32[2,2,16,2048]{3,2,1,0:T(8,128)S(1)}, f32[2,2,16,2048]{3,2,1,0:T(8,128)}, u32[]{:S(2)}) copy-start(f32[2,2,16,2048]{3,2,1,0:T(8,128)} %second.1) | copy-start | bytes 1572868
  0.7 56.5 %copy-start.1 = (f32[2,2,16,2048]{3,2,1,0:T(8,128)S(1)}, f32[2,2,16,2048]{3,2,1,0:T(8,128)}, u32[]{:S(2)}) copy-start(f32[2,2,16,2048]{3,2,1,0:T(8,128)} %first.1) | copy-start | bytes 1572868

commit v5 on v4

--- a/solution.py
+++ b/solution.py
@@ -290,12 +290,12 @@
             gst[q, j, 0, n] = grad_real[j * ROWS : (j + 1) * ROWS]
             gst[q, j, 1, n] = grad_imag[j * ROWS : (j + 1) * ROWS]
 
-    def grad_copy(q, j):
+    def grad_copy(q, j, n):
         return pltpu.make_async_remote_copy(
-            src_ref=gst.at[q, lax.rem(j, SPAN)],
-            dst_ref=out.at[j, me_slab],
-            send_sem=grad_send.at[q, j],
-            recv_sem=grad_recv.at[j, me_slab],
+            src_ref=gst.at[q, lax.rem(j, SPAN), :, n],
+            dst_ref=out.at[j, me_slab, :, n],
+            send_sem=grad_send.at[q, j, n],
+            recv_sem=grad_recv.at[j, me_slab, n],
             device_id=holder(q, j),
             device_id_type=MESH,
         )
@@ -304,17 +304,17 @@
         gst.at[me_slab, CENTER], out.at[CENTER, me_slab], own_sem
     )
 
-    def send_grads(q):
+    def send_grads(q, n):
         def one(j, carry):
             @pl.when(remote(q, j))
             def _():
-                grad_copy(q, j).start()
+                grad_copy(q, j, n).start()
 
             return carry
 
         lax.fori_loop(0, REACH, one, 0)
 
-        @pl.when(q == me_slab)
+        @pl.when((q == me_slab) & (n == 0))
         def _():
             own_copy.start()
 
@@ -322,9 +322,7 @@
         s = slices - 1 - i
         leave(s)
 
-        @pl.when(lax.rem(s, 2) == 0)
-        def _():
-            send_grads(s // 2)
+        send_grads(s // 2, lax.rem(s, 2))
 
         real, imag = waves[0], waves[1]
         layer_real, layer_imag = layer(s)
@@ -339,7 +337,7 @@
 
     lax.fori_loop(0, slices - 1, backward, 0, unroll=True)
     leave(0)
-    send_grads(0)
+    send_grads(0, 0)
 
     def finish_patch(i, carry):
         j, peer = patch_order(i)
@@ -358,15 +356,16 @@
 
         @pl.when(remote(q, j))
         def _():
-            grad_copy(q, j).wait_send()
-            pltpu.make_async_remote_copy(
-                src_ref=gst.at[q, 0],
-                dst_ref=out.at[j, q],
-                send_sem=grad_send.at[q, j],
-                recv_sem=grad_recv.at[j, q],
-                device_id=worker(q, j),
-                device_id_type=MESH,
-            ).wait_recv()
+            for n in range(2):
+                grad_copy(q, j, n).wait_send()
+                pltpu.make_async_remote_copy(
+                    src_ref=gst.at[q, 0, :, n],
+                    dst_ref=out.at[j, q, :, n],
+                    send_sem=grad_send.at[q, j, n],
+                    recv_sem=grad_recv.at[j, q, n],
+                    device_id=worker(q, j),
+                    device_id_type=MESH,
+                ).wait_recv()
 
         return carry
 
@@ -457,8 +456,8 @@
             pltpu.SemaphoreType.DMA((2,)),
             pltpu.SemaphoreType.DMA((count,)),
             pltpu.SemaphoreType.DMA((slabs, REACH)),
-            pltpu.SemaphoreType.DMA((slabs, REACH)),
-            pltpu.SemaphoreType.DMA((REACH, slabs)),
+            pltpu.SemaphoreType.DMA((slabs, REACH, 2)),
+            pltpu.SemaphoreType.DMA((REACH, slabs, 2)),
             pltpu.SemaphoreType.DMA(()),
         ],
         compiler_params=pltpu.CompilerParams(

time: 60 us -> 60.9 us (1.015)
  Pallas kernels: 58.4 us -> 59.3 us
    pallas_call x1, Pallas kernels: 55.7 us -> 56.6 us  [shards(): pl.pallas_call(functools.partial(wave_kernel, slabs, strips), out_shape=p...]
where the time goes in v5:
time: 60.9 us; the launch traced here: 60.8 us
  Pallas kernels  59.3 us (97%)
  between operations  1.46 us (2%)
    pallas_call x1, Pallas kernels, shards(): pl.pallas_call(functools.partial(wave_kernel, slabs, strips), out_shape=p...  56.6 us
    pallas_call x1, Pallas kernels, shards(): pl.pallas_call(functools.partial(update_kernel, slabs, strips), out_shape...  2.7 us

profile of v5, /device:TPU:1, one launch (start us, length us, event | category | flops | bytes accessed | tf_op | source)
XLA Modules:
  0.0 60.8 jit_solution(17889991535394066491)
XLA Ops:
  0.6 0.0 copy-start
  0.6 0.0 copy-start.3
  0.7 0.0 copy-start.2
  0.7 0.0 copy-start.1
  1.4 56.6 %shard_map.103.pieces = f32[9,4,2,2,16,128]{5,4,3,2,1,0:T(8,128)S(1)} custom-call(s32[2,256]{1,0:T(2,128)} %bitcast.1, f32[1]{0:T(128)S(6)} %copy.11.fresnel_in, f32[2,2,16,2048]{3,2,1,0:T(8,128)} %obj.1, f32[2,128,128]{2,1,0:T(8,128)} %probe_in.1, f32[4,128,128]{2,1,0:T(8,128)} %meas_in.1, f32[2,128,128]{2,1,0:T(8,128)} %constant.2.clone.four_in), custom_call_target="tpu_custom_call" | custom-call | tf_op jit(solution)/shard_map/pallas_call | solution.py:436
  58.0 0.0 copy-done
  58.0 0.0 copy-done.3
  58.1 0.0 copy-done.2
  58.1 0.0 copy-done.1
  58.1 2.7 %shard_map.104 = (f32[2,2,16,2048]{3,2,1,0:T(8,128)}, f32[2,2,16,2048]{3,2,1,0:T(8,128)}, f32[2,2,16,2048]{3,2,1,0:T(8,128)}) custom-call(s32[2,256]{1,0:T(2,128)S(1)} %bitcast.2, f32[9,4,2,2,16,128]{5,4,3,2,1,0:T(8,128)S(1)} %shard_map.103.pieces, f32[2,2,16,2048]{3,2,1,0:T(8,128)S(1)} %copy-done, f32[2,2,16,2048]{3,2,1,0:T(8,128)S(1)} %copy-done.1, ...), custom_call_target="tpu_custom_call" | custom-call | tf_op jit(solution)/shard_map/pallas_call | solution.py:468
Async XLA Ops:
  0.6 57.4 %copy-start = (f32[2,2,16,2048]{3,2,1,0:T(8,128)S(1)}, f32[2,2,16,2048]{3,2,1,0:T(8,128)}, u32[]{:S(2)}) copy-start(f32[2,2,16,2048]{3,2,1,0:T(8,128)} %obj.1) | copy-start | bytes 1572868
  0.6 57.4 %copy-start.3 = (s32[256,2]{0,1:T(2,128)S(1)}, s32[256,2]{0,1:T(2,128)}, u32[]{:S(2)}) copy-start(s32[256,2]{0,1:T(2,128)} %param.13) | copy-start | bytes 6148
  0.7 57.4 %copy-start.2 = (f32[2,2,16,2048]{3,2,1,0:T(8,128)S(1)}, f32[2,2,16,2048]{3,2,1,0:T(8,128)}, u32[]{:S(2)}) copy-start(f32[2,2,16,2048]{3,2,1,0:T(8,128)} %second.1) | copy-start | bytes 1572868
  0.7 57.4 %copy-start.1 = (f32[2,2,16,2048]{3,2,1,0:T(8,128)S(1)}, f32[2,2,16,2048]{3,2,1,0:T(8,128)}, u32[]{:S(2)}) copy-start(f32[2,2,16,2048]{3,2,1,0:T(8,128)} %first.1) | copy-start | bytes 1572868
